TPU v7x, 32 devices: a whole 2x2x4 slice. The times are simulated.
32 devices in a mesh: dp: 32 (over z, y, x, core).
Axes of the slice: x: 2, y: 2, z: 4, core: 2. Of those that a mesh axis runs over, the one named last changes fastest.
Arguments:
- local_grads: bfloat16 [32, 32768, 512], P('dp')
- master: float32 [32768, 512], P('dp')
- mom_first: float32 [32768, 512], P('dp')
- mom_second: float32 [32768, 512], P('dp')
- learn_rate: float32 [], replicated
Outputs:
- output 1: float32 [32768, 512], P('dp')
- output 2: float32 [32768, 512], P('dp')
- output 3: float32 [32768, 512], P('dp')
- output 4: bfloat16 [32768, 512], replicated
All inputs are finite; a program needn't handle non-finite values.
Results may differ from a plain program's by a relative error of at most 0.001.
Values are sent between devices in bfloat16 or wider.
A program may use at most 1 GiB of HBM per device.

v0:
```python
import jax
import jax.numpy as jnp
from jax import lax
from jax.sharding import PartitionSpec as P, NamedSharding

LAYERS = 2
MIX_RANK = 32
DECAY_RANK = 64
ADAM_STEP = 10


def layout_runs(model_width, total_rows):
    ffn_width = 7 * model_width // 2
    layer_rows = 6 * model_width + 2 * ffn_width + 16 + 10 * MIX_RANK + 2 * DECAY_RANK
    vocab_rows = (total_rows - LAYERS * layer_rows - 4) // 2
    base_rule = (1.0, 0.0)
    decay_rule = (1.0, 0.1)
    time_rule = (2.0, 0.0)
    pieces = [(vocab_rows, decay_rule)]
    for layer_idx in range(LAYERS):
        lead_rows = 12 if layer_idx == 0 else 10
        pieces = pieces + [(lead_rows + 10 * MIX_RANK, base_rule), (1, time_rule), (2 * DECAY_RANK, base_rule), (1, time_rule), (5 * model_width, decay_rule), (4, base_rule), (2 * ffn_width + model_width, decay_rule)]
    pieces = pieces + [(2, base_rule), (vocab_rows, decay_rule)]
    run_starts = []
    next_row = 0
    for run_len, run_rule in pieces:
        run_starts.append(next_row)
        next_row = next_row + run_len
    lr_values = [run_rule[0] for run_len, run_rule in pieces]
    decay_values = [run_rule[1] for run_len, run_rule in pieces]
    return run_starts, lr_values, decay_values


def row_rules(row_ids, model_width, total_rows):
    run_starts, lr_values, decay_values = layout_runs(model_width, total_rows)
    later_starts = jnp.asarray(run_starts[1:], jnp.int32)
    run_index = jnp.sum((row_ids[:, None] >= later_starts[None, :]).astype(jnp.int32), axis=1)
    lr_factor = jnp.asarray(lr_values, jnp.float32)[run_index]
    decay_rate = jnp.asarray(decay_values, jnp.float32)[run_index]
    return lr_factor[:, None], decay_rate[:, None]


def adam_rows(grad_rows, master_rows, first_rows, second_rows, clip_scale, learn_rate, lr_factor, decay_rate):
    clipped = grad_rows * clip_scale
    new_first = 0.9 * first_rows + 0.1 * clipped
    new_second = 0.99 * second_rows + 0.01 * (clipped * clipped)
    first_hat = new_first / (1.0 - 0.9 ** ADAM_STEP)
    second_hat = new_second / (1.0 - 0.99 ** ADAM_STEP)
    step_size = learn_rate * lr_factor
    new_master = master_rows - step_size * (first_hat / (jnp.sqrt(second_hat) + 1e-8) + decay_rate * master_rows)
    return new_master, new_first, new_second


def solution(mesh):
    dev_count = mesh.shape['dp']

    def device_step(local_grads, master, mom_first, mom_second, learn_rate):
        shard_rows = master.shape[0]
        model_width = master.shape[1]
        total_rows = shard_rows * dev_count
        grad_shard = lax.psum_scatter(local_grads[0].astype(jnp.float32), 'dp', scatter_dimension=0, tiled=True) / dev_count
        square_sum = lax.psum(jnp.sum(grad_shard * grad_shard), 'dp')
        clip_scale = jnp.minimum(1.0, 1.0 / (jnp.sqrt(square_sum) + 1e-6))
        row_ids = lax.axis_index('dp') * shard_rows + lax.iota(jnp.int32, shard_rows)
        lr_factor, decay_rate = row_rules(row_ids, model_width, total_rows)
        new_master, new_first, new_second = adam_rows(grad_shard, master, mom_first, mom_second, clip_scale, learn_rate, lr_factor, decay_rate)
        working = lax.all_gather(new_master.astype(jnp.bfloat16), 'dp', axis=0, tiled=True)
        return new_master, new_first, new_second, working

    return jax.shard_map(device_step, mesh=mesh, in_specs=(P('dp', None, None), P('dp', None), P('dp', None), P('dp', None), P()), out_specs=(P('dp', None), P('dp', None), P('dp', None), P(None, None)), check_vma=False)
```

profile of v0, /device:TPU:0, one launch (start us, length us, event | category | flops | bytes accessed | tf_op | source)
XLA Modules:
  0.0 1025.6 jit_solution(13691135546559383229)
XLA Ops:
  7.2 0.0 reduce-scatter.2.cloned.1.call-start
  7.2 32.4 %bitcast_convert_fusion = f32[32768,512]{1,0:T(8,128)} fusion(bf16[1,32768,512]{2,1,0:T(8,128)(2,1)} %param.8), kind=kLoop, calls=%fused_computation | loop fusion | flops 16777216 | bytes 100663296 | tf_op jit(solution)/shard_map/convert_element_type | solution.py:61
  39.6 0.0 copy-start.1
  39.6 0.0 reduce-scatter.2.cloned.1.call-update
  39.7 0.0 all-gather.2.cloned.1.call-start
  40.4 0.0 copy-done.1
  40.4 0.1 convert_reduce_fusion
  40.5 0.1 compare_reduce_fusion.9
  40.6 704.6 %reduce-scatter.2.cloned.1.call-done = f32[1024,512]{1,0:T(8,128)} async-done(((f32[32768,512]{1,0:T(8,128)}), f32[1024,512]{1,0:T(8,128)}) %reduce-scatter.2.cloned.1.call-update) | async-done | bytes 2097168 | tf_op jit(solution)/shard_map/reduce_scatter | solution.py:61
  745.2 0.0 copy-start
  745.2 2.9 multiply_reduce_fusion
  748.1 47.1 %psum.7 = f32[]{:T(128)} all-reduce(f32[]{:T(128)} %multiply_reduce_fusion), channel_id=1, replica_groups=mesh['dp'=32] {'dp'}, use_global_device_ids=true, to_apply=%region_3.0 | all-reduce | flops 1 | bytes 8 | tf_op jit(solution)/shard_map/psum | solution.py:62
  795.9 0.0 copy-done
  795.9 6.0 fusion
  801.9 0.0 all-gather.2.cloned.1.call-update
  801.9 193.7 %all-gather.2.cloned.1.call-done = bf16[32768,512]{1,0:T(8,128)(2,1)} async-done(((bf16[1024,512]{1,0:T(8,128)(2,1)}), bf16[32768,512]{1,0:T(8,128)(2,1)}) %all-gather.2.cloned.1.call-update) | async-done | bytes 33554448 | tf_op jit(solution)/shard_map/all_gather | solution.py:67
  995.6 23.2 %copy.14 = bf16[32768,512]{1,0:T(8,128)(2,1)} copy(bf16[32768,512]{1,0:T(8,128)(2,1)} %all-gather.2.cloned.1.call-done) | data formatting | bytes 67108864
  (4 shorter events, 0.1 us)
Async XLA Ops:
  7.2 738.0 %reduce-scatter.2.cloned.1.call-start = ((), (), s32[]{:S(2)}) async-start(), calls=%async_computation.1 | async-start | bytes 69206016 | tf_op jit(solution)/shard_map/reduce_scatter | solution.py:61
  39.6 0.7 copy-start.1
  39.7 955.9 %all-gather.2.cloned.1.call-start = ((), (), s32[]{:S(2)}) async-start(), calls=%async_computation.2 | async-start | bytes 34603008 | tf_op jit(solution)/shard_map/all_gather | solution.py:67
  745.2 50.7 %copy-start = (f32[1024,512]{1,0:T(8,128)S(1)}, f32[1024,512]{1,0:T(8,128)}, u32[]{:S(2)}) copy-start(f32[1024,512]{1,0:T(8,128)} %reduce-scatter.2.cloned.1.call-done) | copy-start | bytes 6291460
Sparse Core Ops, SparseCore 0:
  39.8 705.3 reduce-scatter.1
  802.0 193.5 all-gather.1
where the time goes:
time: 1030 us
  waiting for transfers between devices  898 us (87%)
  blocking collectives  47.1 us (5%)
  other arithmetic  41.5 us (4%)
  local copies, waits for them, and re-layouts  23.2 us (2%)
  between operations  15.5 us (2%)
    reduce_scatter x1, waiting for transfers between devices, device_step(): lax.psum_scatter(local_grads[0].astype(jnp.float32), 'dp', scatter_dimens...  705 us
    all_gather x1, waiting for transfers between devices, device_step(): lax.all_gather(new_master.astype(jnp.bfloat16), 'dp', axis=0, tiled=True)  194 us
    psum x1, blocking collectives, device_step(): square_sum = lax.psum(jnp.sum(grad_shard * grad_shard), 'dp')  47.1 us
    convert_element_type x1, other arithmetic, device_step(): local_grads[0].astype(jnp.float32)  32.4 us
    unnamed x5, local copies, waits for them, and re-layouts  23.2 us
  transfers between devices with their start and end apart: 2, of which 2 were waited for; matrix products, arithmetic and copies ran while one was open for 0% of the time, Pallas kernels for 0%

commit v1 on v0

v1 whole, which is shorter than its diff:
```python
import functools
import jax
import jax.numpy as jnp
from jax import lax
from jax.experimental import pallas as pl
from jax.experimental.pallas import tpu as pltpu
from jax.sharding import PartitionSpec as P

LAYERS = 2
MIX_RANK = 32
DECAY_RANK = 64
ADAM_STEP = 10
STREAMS = 4
MESH = pl.DeviceIdType.MESH

END_JOBS = [
    ("first", 2, 0), ("first", 2, 1), ("first", 3, 1), ("first", 1, 1),
    ("up", 2, 0), ("up", 2, 1), ("pre", 3, 1),
    ("first", 3, 0), ("first", 1, 0), ("first", 0, 1), ("first", 0, 0),
    ("up", 1, 1), ("up", 3, 0), ("up", 1, 0), ("fin", 0, 1), ("res", 0, 0),
]
MID_JOBS = [
    ("first", 3, 1), ("first", 2, 0), ("first", 0, 1), ("first", 2, 1),
    ("up", 3, 1),
    ("first", 3, 0), ("first", 1, 1), ("first", 0, 0), ("first", 1, 0),
    ("up", 2, 0), ("down", 0, 1), ("up", 2, 1), ("fin", 1, 1), ("up", 3, 0), ("down", 0, 0), ("res", 1, 0),
]
END_EVENTS = [(0, 1, "u"), (1, 0, ""), (2, 0, ""), (3, 0, "q"), (1, 1, ""), (3, 1, ""), (2, 1, "")]
MID_EVENTS = [(2, 0, "d"), (0, 0, "u"), (1, 1, "u"), (0, 1, "u"), (3, 0, "de"), (2, 1, "d"), (3, 1, "")]


def rule_runs(model_width, total_rows):
    ffn_width = 7 * model_width // 2
    layer_rows = 6 * model_width + 2 * ffn_width + 16 + 10 * MIX_RANK + 2 * DECAY_RANK
    vocab_rows = (total_rows - LAYERS * layer_rows - 4) // 2
    decay_runs = [(0, vocab_rows)]
    fast_rows = []
    row = vocab_rows
    for layer_idx in range(LAYERS):
        row = row + (12 if layer_idx == 0 else 10) + 10 * MIX_RANK
        fast_rows.append(row)
        row = row + 1 + 2 * DECAY_RANK
        fast_rows.append(row)
        row = row + 1
        decay_runs.append((row, row + 5 * model_width))
        row = row + 5 * model_width + 4
        decay_runs.append((row, row + 2 * ffn_width + model_width))
        row = row + 2 * ffn_width + model_width
    row = row + 2
    decay_runs.append((row, row + vocab_rows))
    return decay_runs, fast_rows


def step_kernel(
    lr_ref, grads, master, mom1, mom2,
    o_master, o_mom1, o_mom2, o_work, praw,
    stg, acc, zd, zu, pre, fin, rb, wbuf, nsum, nb, nr,
    core_s, core_r, first_s, first_r, z_s, zd_r, zu_r, q_s, pre_r, fin_r,
    ld, st_ld, st_out, own_out, norm_s, norm_r,
    gat_r, gcore_r, gcore_s, gp_s, gup_s, gdn_s, gq_s,
):
    rows, width = acc.shape[2], acc.shape[3]
    shard = STREAMS * rows
    total_rows = grads.shape[1]
    tile = min(32, rows)
    me = lax.axis_index("dp")
    c, x, y, z = me % 2, (me // 2) % 2, (me // 4) % 2, me // 8
    lo = 1 - z // 2
    m = lo * z + (1 - lo) * (3 - z)
    sgn = 2 * lo - 1

    def dev(zz, yy, xx, cc):
        return ((zz * 2 + yy) * 2 + xx) * 2 + cc

    partner = dev(z, y, x, 1 - c)
    xn, yn = dev(z, y, 1 - x, c), dev(z, 1 - y, x, c)
    up = dev(z + sgn, y, x, c)
    down = dev(z - sgn, y, x, c)
    zothers = [dev((z + d) % 4, y, x, c) for d in (1, 2, 3)]

    def pn(s):
        h = s % 2
        return xn * (1 - h) + yn * h

    def qn(s):
        h = s % 2
        return yn * (1 - h) + xn * h

    def chip(s, u, qo, po):
        h = s % 2
        first = x * (1 - h) + y * h
        last = y * (1 - h) + x * h
        pv = 1 - first if po else first
        qv = 1 - last if qo else last
        xx = pv * (1 - h) + qv * h
        yy = qv * (1 - h) + pv * h
        return ((lo * u + (1 - lo) * (3 - u)) * 2 + yy) * 2 + xx

    def remote(src, dst, ssem, rsem, to):
        return pltpu.make_async_remote_copy(
            src_ref=src, dst_ref=dst, send_sem=ssem, recv_sem=rsem, device_id=(to,), device_id_type=MESH
        )

    def each(n, body):
        def step(i, carry):
            body(i)
            return carry

        lax.fori_loop(0, n, step, 0)

    barrier = pltpu.get_barrier_semaphore()
    for other in [partner, xn, yn] + zothers:
        pl.semaphore_signal(barrier, inc=1, device_id=(other,), device_id_type=MESH)
    pl.semaphore_wait(barrier, 6)

    def grad_rows(ci, s, cc):
        return grads.at[0, pl.ds(pl.multiple_of((ci * 2 + cc) * shard + s * rows, rows), rows)]

    def praw_rows(ci, s):
        return praw.at[pl.ds(pl.multiple_of((ci * STREAMS + s) * rows, rows), rows)]

    def core_copy(ci, s):
        i = ci * STREAMS + s
        return remote(grad_rows(ci, s, 1 - c), praw_rows(ci, s), core_s.at[i], core_r.at[i], partner)

    def loads(job, slot, s):
        ci = chip(s, job[1], job[2], job[0] == "first")
        own = pltpu.make_async_copy(grad_rows(ci, s, c), rb.at[slot, s, 0], ld.at[slot, s, 0])
        other = pltpu.make_async_copy(praw_rows(ci, s), rb.at[slot, s, 1], ld.at[slot, s, 1])
        return ci, own, other

    def prefetch(job, slot):
        def body(s):
            ci, own, other = loads(job, slot, s)
            core_copy(ci, s).wait_recv()
            own.start()
            other.start()

        each(STREAMS, body)

    def landed(ref, rsem):
        remote(ref, ref, z_s.at[0, 0], rsem, me).wait_recv()

    def sent(ref, ssem):
        remote(ref, ref, ssem, zu_r.at[0, 0], me).wait_send()

    def run_job(job, slot, mid, zslot):
        kind, u, qo = job
        k = 2 * u + qo

        def body(s):
            _, own, other = loads(job, slot, s)
            parts = []
            if kind != "first":
                parts.append((acc.at[s, k], first_r.at[s, k]))
                from_down = mid and u >= 1 and not (u == 3 and qo == 1)
                from_up = (mid and u <= 1) or (not mid and u == 0)
                if from_down:
                    parts.append((zd.at[s, k - 2], zd_r.at[s, k - 2]))
                if from_up:
                    parts.append((zu.at[s, k], zu_r.at[s, k]))
                if not mid and (u, qo) == (3, 0):
                    parts.append((pre.at[s], pre_r.at[s]))
                if kind == "res":
                    parts.append((fin.at[s], fin_r.at[s]))
            for ref, rsem in parts:
                landed(ref, rsem)
            own.wait()
            other.wait()
            dst = stg.at[s, k] if kind == "first" else acc.at[s, k]

            def add(t):
                at = pl.ds(pl.multiple_of(t * tile, tile), tile)
                v = rb[slot, s, 0, at, :].astype(jnp.float32) + rb[slot, s, 1, at, :].astype(jnp.float32)
                for ref, _ in parts:
                    v = v + ref[at, :]
                if kind == "res":
                    v = v * (1.0 / 32.0)
                    nsum[...] += jnp.sum((v * v).reshape(tile // 8, 8, width), axis=0)
                dst[at, :] = v

            each(rows // tile, add)
            if kind == "first":
                remote(dst, acc.at[s, k], first_s.at[s, k], first_r.at[s, k], pn(s)).start()
            elif kind == "pre":
                remote(dst, pre.at[s], q_s.at[s, 0], pre_r.at[s], qn(s)).start()
            elif kind == "fin":
                remote(dst, fin.at[s], q_s.at[s, 1], fin_r.at[s], qn(s)).start()
            elif kind == "up" and not mid:
                remote(dst, zd.at[s, k - 2], z_s.at[s, zslot], zd_r.at[s, k - 2], up).start()
            elif kind == "up":
                kk = 2 * (3 - u) + qo
                remote(dst, zu.at[s, kk], z_s.at[s, zslot], zu_r.at[s, kk], up).start()
            elif kind == "down":
                remote(dst, zu.at[s, k], z_s.at[s, zslot], zu_r.at[s, k], down).start()

        each(STREAMS, body)

    def state_load(s):
        at = pl.ds(pl.multiple_of(s * rows, rows), rows)
        return [
            pltpu.make_async_copy(ref.at[at], stg.at[i, s], st_ld.at[i, s])
            for i, ref in enumerate((master, mom1, mom2))
        ]

    def state_store(s):
        at = pl.ds(pl.multiple_of(s * rows, rows), rows)
        return [
            pltpu.make_async_copy(stg.at[i, s], ref.at[at], st_out.at[i, s])
            for i, ref in enumerate((o_master, o_mom1, o_mom2))
        ]

    def reduce_program(jobs, mid):
        order = [j for j in jobs if j[0] == "first"] + [j for j in jobs if j[0] != "first"]
        for kind, u, qo in order:
            each(STREAMS, lambda s: core_copy(chip(s, u, qo, kind == "first"), s).start())
        prefetch(jobs[0], 0)
        zslot = 0
        for j, job in enumerate(jobs):
            if j + 1 < len(jobs):
                prefetch(jobs[j + 1], (j + 1) % 2)
            if job[0] == "res":
                each(8 * STREAMS, lambda i: sent(stg.at[i // 8, i % 8], first_s.at[i // 8, i % 8]))

                def start_state(s):
                    for copy in state_load(s):
                        copy.start()

                each(STREAMS, start_state)
            run_job(job, j % 2, mid, zslot)
            if job[0] in ("up", "down"):
                zslot += 1
        each(zslot * STREAMS, lambda i: sent(acc.at[0, 0], z_s.at[i // zslot, i % zslot]))
        if not mid:
            each(STREAMS, lambda s: sent(acc.at[0, 0], q_s.at[s, 0]))
        each(STREAMS, lambda s: sent(acc.at[0, 0], q_s.at[s, 1]))

    nsum[...] = jnp.zeros_like(nsum)

    @pl.when(m == 0)
    def _():
        reduce_program(END_JOBS, False)

    @pl.when(m == 1)
    def _():
        reduce_program(MID_JOBS, True)

    part = nsum[:, 0:128]
    for col in range(128, width, 128):
        part = part + nsum[:, col:col + 128]
    for i, other in enumerate((partner, xn, yn)):
        nb[i] = part
        copy = remote(nb.at[i], nr.at[i], norm_s.at[i], norm_r.at[i], other)
        copy.start()
        copy.wait()
        part = part + nr[i]
    nb[3] = part
    for i, other in enumerate(zothers):
        remote(nb.at[3], nr.at[3 + i], norm_s.at[3 + i], norm_r.at[3 + i], other).start()
    for i in range(3):
        sent(nb.at[3], norm_s.at[3 + i])
        landed(nr.at[3 + i], norm_r.at[3 + i])
    square_sum = jnp.sum((part + nr[4]) + (nr[3] + nr[5]), keepdims=True)
    clip = jnp.minimum(1.0, 1.0 / (jnp.sqrt(square_sum) + 1e-6))
    clip = jnp.broadcast_to(clip, (tile, 128))

    learn_rate = lr_ref[0]
    inv1 = 1.0 / (1.0 - 0.9 ** ADAM_STEP)
    inv2 = 1.0 / (1.0 - 0.99 ** ADAM_STEP)
    decay_runs, fast_rows = rule_runs(width, total_rows)
    my_chip = me // 2

    def work_rows(ci, s, cc):
        return o_work.at[pl.ds(pl.multiple_of((ci * 2 + cc) * shard + s * rows, rows), rows)]

    def own_store(s):
        return pltpu.make_async_copy(wbuf.at[s], work_rows(my_chip, s, c), own_out.at[s])

    def pass_on(src, ci, s, ssem, to):
        remote(src, work_rows(ci, s, c), ssem, gat_r.at[ci * STREAMS + s], to).start()

    def to_core(src, ci, s):
        i = ci * STREAMS + s
        remote(src, work_rows(ci, s, c), gcore_s.at[i], gcore_r.at[i], partner).start()

    def update(s):
        for copy in state_load(s):
            copy.wait()

        def rows_step(t):
            base = pl.multiple_of(t * tile, tile)
            at = pl.ds(base, tile)
            row = me * shard + s * rows + base + lax.broadcasted_iota(jnp.int32, (tile, 128), 0)
            decays = (row >= decay_runs[0][0]) & (row < decay_runs[0][1])
            for start, stop in decay_runs[1:]:
                decays = decays | ((row >= start) & (row < stop))
            fast = row == fast_rows[0]
            for fast_row in fast_rows[1:]:
                fast = fast | (row == fast_row)
            decay = jnp.where(decays, 0.1, 0.0)
            step_size = learn_rate * jnp.where(fast, 2.0, 1.0)
            for col in range(0, width, 128):
                cols = pl.ds(col, 128)
                g = acc[s, 2 * m, at, cols] * clip
                old = stg[0, s, at, cols]
                first = 0.9 * stg[1, s, at, cols] + 0.1 * g
                second = 0.99 * stg[2, s, at, cols] + 0.01 * (g * g)
                new = old - step_size * ((first * inv1) / (jnp.sqrt(second * inv2) + 1e-8) + decay * old)
                stg[0, s, at, cols] = new
                stg[1, s, at, cols] = first
                stg[2, s, at, cols] = second
                wbuf[s, at, cols] = new.astype(jnp.bfloat16)

        each(rows // tile, rows_step)
        pass_on(wbuf.at[s], my_chip, s, gq_s.at[s, 0], qn(s))
        pass_on(wbuf.at[s], my_chip, s, gup_s.at[s, 0], up)

        @pl.when(m == 1)
        def _():
            pass_on(wbuf.at[s], my_chip, s, gdn_s.at[s, 0], down)

        pass_on(wbuf.at[s], my_chip, s, gp_s.at[s, 0], pn(s))
        to_core(wbuf.at[s], my_chip, s)
        own_store(s).start()
        for copy in state_store(s):
            copy.start()

    each(STREAMS, update)

    def arrive(s, u, qo, po):
        ci = chip(s, u, qo, po)
        ref = work_rows(ci, s, c)
        landed(ref, gat_r.at[ci * STREAMS + s])
        return ci, ref

    def gather_program(events, own):
        passed = [(own, 0)]
        ups, downs = 1, 1
        for n, (u, qo, links) in enumerate(events):
            def event(s, ups=ups, downs=downs):
                ci, ref = arrive(s, u, qo, 0)
                if "u" in links:
                    pass_on(ref, ci, s, gup_s.at[s, ups], up)
                if "d" in links:
                    pass_on(ref, ci, s, gdn_s.at[s, downs], down)
                if "e" in links:
                    ce = chip(s, 1, 1, 0)
                    pass_on(work_rows(ce, s, c), ce, s, gdn_s.at[s, downs + 1], down)
                if "q" in links:
                    pass_on(ref, ci, s, gq_s.at[s, 1], qn(s))
                pass_on(ref, ci, s, gp_s.at[s, n + 1], pn(s))
                to_core(ref, ci, s)

            each(STREAMS, event)
            ups += links.count("u")
            downs += links.count("d") + links.count("e")
            passed.append((u, qo))
            if n >= 1:
                other_side(*passed[n - 1])
        for u, qo in passed[len(events) - 1:]:
            other_side(u, qo)
        mid = own == 1
        block = wbuf.at[0]
        each(ups * STREAMS, lambda i: sent(block, gup_s.at[i // ups, i % ups]))
        if mid:
            each(downs * STREAMS, lambda i: sent(block, gdn_s.at[i // downs, i % downs]))
        else:
            each(STREAMS, lambda s: sent(block, gq_s.at[s, 1]))

    def other_side(u, qo):
        def body(s):
            ci, ref = arrive(s, u, qo, 1)
            to_core(ref, ci, s)

        each(STREAMS, body)

    @pl.when(m == 0)
    def _():
        gather_program(END_EVENTS, 0)

    @pl.when(m == 1)
    def _():
        gather_program(MID_EVENTS, 1)

    block = wbuf.at[0]

    def drain(s):
        sent(block, gq_s.at[s, 0])
        own_store(s).wait()
        for copy in state_store(s):
            copy.wait()

    each(STREAMS, drain)
    each(8 * STREAMS, lambda i: sent(block, gp_s.at[i // 8, i % 8]))

    def drain_core(i):
        ci, s = i // STREAMS, i % STREAMS
        core_copy(ci, s).wait_send()
        sent(block, gcore_s.at[i])
        landed(work_rows(ci, s, 1 - c), gcore_r.at[i])

    each(16 * STREAMS, drain_core)


def solution(mesh):
    dev_count = mesh.shape["dp"]

    def device_step(local_grads, master, mom_first, mom_second, learn_rate):
        shard_rows, width = master.shape
        total_rows = shard_rows * dev_count
        rows = shard_rows // STREAMS
        any_spec = pl.BlockSpec(memory_space=pl.ANY)
        dma = pltpu.SemaphoreType.DMA
        f32, bf16 = jnp.float32, jnp.bfloat16
        shard = jax.ShapeDtypeStruct((shard_rows, width), f32)
        outs = pl.pallas_call(
            step_kernel,
            out_shape=[
                shard, shard, shard,
                jax.ShapeDtypeStruct((total_rows, width), bf16),
                jax.ShapeDtypeStruct((total_rows // 2, width), bf16),
            ],
            in_specs=[pl.BlockSpec(memory_space=pltpu.SMEM)] + [any_spec] * 4,
            out_specs=[any_spec] * 5,
            scratch_shapes=[
                pltpu.VMEM((STREAMS, 8, rows, width), f32),
                pltpu.VMEM((STREAMS, 8, rows, width), f32),
                pltpu.VMEM((STREAMS, 5, rows, width), f32),
                pltpu.VMEM((STREAMS, 4, rows, width), f32),
                pltpu.VMEM((STREAMS, rows, width), f32),
                pltpu.VMEM((STREAMS, rows, width), f32),
                pltpu.VMEM((2, STREAMS, 2, rows, width), bf16),
                pltpu.VMEM((STREAMS, rows, width), bf16),
                pltpu.VMEM((8, width), f32),
                pltpu.VMEM((4, 8, 128), f32),
                pltpu.VMEM((6, 8, 128), f32),
                dma((16 * STREAMS,)), dma((16 * STREAMS,)),
                dma((STREAMS, 8)), dma((STREAMS, 8)),
                dma((STREAMS, 6)), dma((STREAMS, 5)), dma((STREAMS, 4)),
                dma((STREAMS, 2)), dma((STREAMS,)), dma((STREAMS,)),
                dma((2, STREAMS, 2)), dma((3, STREAMS)), dma((3, STREAMS)), dma((STREAMS,)),
                dma((6,)), dma((6,)),
                dma((16 * STREAMS,)), dma((16 * STREAMS,)), dma((16 * STREAMS,)),
                dma((STREAMS, 8)), dma((STREAMS, 4)), dma((STREAMS, 5)), dma((STREAMS, 2)),
            ],
            compiler_params=pltpu.CompilerParams(
                collective_id=0, has_side_effects=True, vmem_limit_bytes=67043328
            ),
            name="adam_step",
        )(learn_rate.reshape(1), local_grads, master, mom_first, mom_second)
        return outs[0], outs[1], outs[2], outs[3]

    return jax.shard_map(
        device_step,
        mesh=mesh,
        in_specs=(P("dp", None, None), P("dp", None), P("dp", None), P("dp", None), P()),
        out_specs=(P("dp", None), P("dp", None), P("dp", None), P(None, None)),
        check_vma=False,
    )
```

time: 1030 us -> 423 us (0.41)
  waiting for transfers between devices: 898 us -> 0 us
  Pallas kernels: 0 us -> 392 us
  blocking collectives: 47.1 us -> 0 us
  other arithmetic: 41.5 us -> 0 us
  between operations: 15.5 us -> 1.3 us
    reduce_scatter x1 -> x0, waiting for transfers between devices: 705 us -> none  [device_step(): lax.psum_scatter(local_grads[0].astype(jnp.float32), 'dp', scatter_dimens...]
    pallas_call x0 -> x1, Pallas kernels: none -> 392 us  [device_step(): pl.pallas_call(step_kernel, out_shape=[shard, shard, shard, jax.ShapeDtyp...]
    all_gather x1 -> x0, waiting for transfers between devices: 194 us -> none  [device_step(): lax.all_gather(new_master.astype(jnp.bfloat16), 'dp', axis=0, tiled=True)]
    psum x1 -> x0, blocking collectives: 47.1 us -> none  [device_step(): square_sum = lax.psum(jnp.sum(grad_shard * grad_shard), 'dp')]
    convert_element_type x2 -> x0, other arithmetic: 38.4 us -> none  [the longest x1 32.4 us: device_step(): local_grads[0].astype(jnp.float32)]
    unnamed x5 -> x8, local copies, waits for them, and re-layouts: 23.2 us -> 29.8 us
  transfers between devices with their start and end apart: 2 -> 0, of which waited for: 2 -> 0; matrix products, arithmetic and copies ran while one was open for 0% -> 0% of each run, Pallas kernels for 0% -> 0%
where the time goes in v1:
time: 423 us
  Pallas kernels  392 us (93%)
  local copies, waits for them, and re-layouts  29.8 us (7%)
    pallas_call x1, Pallas kernels, device_step(): pl.pallas_call(step_kernel, out_shape=[shard, shard, shard, jax.ShapeDtyp...  392 us
    unnamed x8, local copies, waits for them, and re-layouts  29.8 us

profile of v1, /device:TPU:0, one launch (start us, length us, event | category | flops | bytes accessed | tf_op | source)
XLA Modules:
  0.0 423.2 jit_solution(5138873394731068232)
XLA Ops:
  1.3 392.1 %adam_step.1 = (f32[1024,512]{1,0:T(8,128)}, f32[1024,512]{1,0:T(8,128)}, f32[1024,512]{1,0:T(8,128)}, bf16[32768,512]{1,0:T(8,128)(2,1)}, bf16[16384,512]{1,0:T(8,128)(2,1)}) custom-call(f32[1]{0:T(128)} %bitcast.1.lr_ref, bf16[1,32768,512]{2,1,0:T(8,128)(2,1)} %grads.1, f32[1024,512]{1,0:T(8,128)} %master.1, f32[1024,512]{1,0:T(8,128)} %mom1.1, ...), custom_call_target="tpu_custom_call" | custom-call | tf_op jit(solution)/shard_map/adam_step/pallas_call | solution.py:416
  393.4 0.0 copy-start.1
  393.4 3.2 copy.14
  396.7 0.0 copy-done.1
  396.7 0.0 copy-start
  396.7 1.3 copy.15
  398.0 1.0 copy-done
  399.0 1.3 copy.16
  400.3 22.9 %copy.17 = bf16[32768,512]{1,0:T(8,128)(2,1)} copy(bf16[32768,512]{1,0:T(8,128)(2,1)} %get-tuple-element.19) | data formatting | bytes 67108864
Async XLA Ops:
  393.4 3.2 copy-start.1
  396.7 2.3 copy-start

commit v2 on v0

v2 whole, which is shorter than its diff:
```python
import jax
import jax.numpy as jnp
from jax import lax
from jax.experimental import pallas as pl
from jax.experimental.pallas import tpu as pltpu
from jax.sharding import PartitionSpec as P

LAYERS = 2
MIX_RANK = 32
DECAY_RANK = 64
ADAM_STEP = 10
STREAMS = 8
GROUP = 4
MESH = pl.DeviceIdType.MESH

END_JOBS = [
    ("first", 2, 0, 1), ("first", 2, 1, 1), ("first", 2, 0, 0), ("first", 3, 1, 1), ("up", 2, 0, 1),
    ("up", 2, 1, 1), ("first", 1, 1, 1), ("first", 1, 0, 0), ("up", 1, 1, 1), ("first", 2, 1, 0),
    ("first", 3, 1, 0), ("up", 2, 1, 0), ("pre", 3, 1, 0), ("first", 1, 1, 0), ("first", 3, 0, 0),
    ("up", 2, 0, 0), ("up", 1, 1, 0), ("pre", 3, 1, 1), ("first", 0, 1, 0), ("first", 3, 0, 1),
    ("first", 0, 1, 1), ("up", 3, 0, 0), ("up", 3, 0, 1), ("first", 1, 0, 1), ("fin", 0, 1, 1),
    ("fin", 0, 1, 0), ("up", 1, 0, 0), ("first", 0, 0, 0), ("first", 0, 0, 1), ("up", 1, 0, 1),
    ("res", 0, 0, 0), ("res", 0, 0, 1),
]
MID_JOBS = [
    ("first", 3, 1, 0), ("first", 3, 1, 1), ("first", 2, 0, 1), ("first", 1, 0, 1), ("up", 2, 0, 1),
    ("up", 3, 1, 1), ("first", 2, 1, 0), ("first", 2, 1, 1), ("first", 0, 1, 0), ("first", 1, 1, 0),
    ("first", 3, 0, 1), ("first", 0, 1, 1), ("up", 3, 1, 0), ("first", 3, 0, 0), ("up", 2, 1, 0),
    ("first", 1, 1, 1), ("up", 2, 1, 1), ("first", 0, 0, 0), ("first", 0, 0, 1), ("down", 0, 1, 0),
    ("first", 2, 0, 0), ("down", 0, 1, 1), ("up", 3, 0, 0), ("down", 0, 0, 0), ("up", 3, 0, 1),
    ("fin", 1, 1, 0), ("first", 1, 0, 0), ("fin", 1, 1, 1), ("down", 0, 0, 1), ("up", 2, 0, 0),
    ("res", 1, 0, 0), ("res", 1, 0, 1),
]
END_SENDS = [
    (0, 0, 0, "q", 0), (0, 0, 0, "q", 1), (0, 0, 0, "u", 0), (0, 0, 0, "u", 1), (0, 0, 0, "p", 0),
    (0, 0, 0, "p", 1), (0, 0, 0, "c", 0), (0, 0, 0, "c", 1), (1, 0, 0, "p", 1), (0, 1, 0, "u", 0),
    (0, 0, 1, "c", 1), (0, 1, 0, "u", 1), (0, 1, 0, "p", 1), (1, 0, 0, "p", 0), (3, 0, 0, "p", 0),
    (1, 0, 0, "c", 1), (3, 0, 0, "c", 0), (0, 1, 0, "p", 0), (3, 0, 0, "q", 0), (3, 0, 0, "q", 1),
    (2, 0, 0, "c", 0), (3, 1, 0, "c", 0), (2, 0, 0, "p", 0), (3, 0, 0, "c", 1), (0, 1, 0, "c", 1),
    (0, 1, 1, "c", 0), (3, 0, 0, "p", 1), (2, 0, 0, "p", 1), (0, 1, 0, "c", 0), (3, 1, 0, "p", 0),
    (3, 0, 1, "c", 0), (2, 1, 0, "p", 0), (2, 0, 1, "c", 1), (3, 0, 1, "c", 1), (2, 0, 0, "c", 1),
    (3, 1, 0, "c", 1), (1, 1, 0, "p", 1), (3, 1, 0, "p", 1), (0, 0, 1, "c", 0), (2, 1, 0, "p", 1),
    (1, 1, 0, "c", 1), (2, 1, 0, "c", 0), (1, 1, 1, "c", 1), (0, 1, 1, "c", 1), (1, 0, 1, "c", 1),
    (2, 0, 1, "c", 0), (2, 1, 0, "c", 1), (3, 1, 1, "c", 1), (2, 1, 1, "c", 0), (3, 1, 1, "c", 0),
    (1, 0, 0, "c", 0), (1, 1, 0, "p", 0), (2, 1, 1, "c", 1), (1, 1, 0, "c", 0), (1, 0, 1, "c", 0),
    (1, 1, 1, "c", 0),
]
MID_SENDS = [
    (1, 0, 0, "q", 0), (1, 0, 0, "q", 1), (1, 0, 0, "u", 0), (1, 0, 0, "u", 1), (1, 0, 0, "d", 0),
    (1, 0, 0, "d", 1), (1, 0, 0, "p", 0), (1, 0, 0, "p", 1), (1, 0, 0, "c", 0), (1, 0, 0, "c", 1),
    (2, 0, 0, "d", 0), (0, 0, 0, "u", 0), (0, 0, 0, "p", 1), (2, 0, 0, "c", 1), (2, 0, 0, "p", 1),
    (2, 0, 0, "p", 0), (0, 0, 0, "u", 1), (3, 0, 0, "d", 0), (1, 1, 0, "u", 0), (0, 1, 0, "p", 0),
    (1, 1, 0, "u", 1), (1, 1, 0, "p", 1), (3, 0, 0, "p", 0), (3, 0, 0, "d", 1), (0, 1, 0, "p", 1),
    (2, 0, 0, "c", 0), (2, 0, 0, "d", 1), (1, 1, 0, "d", 1), (0, 1, 0, "u", 1), (2, 1, 0, "d", 0),
    (0, 1, 0, "c", 0), (0, 1, 0, "u", 0), (0, 0, 0, "p", 0), (2, 0, 1, "c", 0), (3, 0, 1, "c", 0),
    (2, 1, 0, "p", 1), (1, 1, 0, "p", 0), (0, 0, 0, "c", 0), (2, 1, 0, "d", 1), (2, 1, 1, "c", 1),
    (1, 1, 0, "c", 0), (2, 0, 1, "c", 1), (2, 1, 0, "p", 0), (3, 1, 0, "p", 1), (1, 1, 1, "c", 0),
    (3, 0, 0, "c", 1), (0, 1, 1, "c", 1), (1, 1, 0, "c", 1), (2, 1, 0, "c", 1), (0, 1, 1, "c", 0),
    (1, 1, 0, "d", 0), (3, 1, 0, "c", 1), (0, 0, 1, "c", 1), (3, 1, 0, "p", 0), (3, 0, 0, "p", 1),
    (0, 0, 0, "c", 1), (0, 0, 1, "c", 0), (2, 1, 0, "c", 0), (1, 1, 1, "c", 1), (3, 1, 1, "c", 1),
    (1, 0, 1, "c", 1), (0, 1, 0, "c", 1), (2, 1, 1, "c", 0), (3, 0, 0, "c", 0), (1, 0, 1, "c", 0),
    (3, 1, 0, "c", 0), (3, 1, 1, "c", 0), (3, 0, 1, "c", 1),
]


def rule_runs(model_width, total_rows):
    ffn_width = 7 * model_width // 2
    layer_rows = 6 * model_width + 2 * ffn_width + 16 + 10 * MIX_RANK + 2 * DECAY_RANK
    vocab_rows = (total_rows - LAYERS * layer_rows - 4) // 2
    decay_runs = [(0, vocab_rows)]
    fast_rows = []
    row = vocab_rows
    for layer_idx in range(LAYERS):
        row = row + (12 if layer_idx == 0 else 10) + 10 * MIX_RANK
        fast_rows.append(row)
        row = row + 1 + 2 * DECAY_RANK
        fast_rows.append(row)
        row = row + 1
        decay_runs.append((row, row + 5 * model_width))
        row = row + 5 * model_width + 4
        decay_runs.append((row, row + 2 * ffn_width + model_width))
        row = row + 2 * ffn_width + model_width
    row = row + 2
    decay_runs.append((row, row + vocab_rows))
    return decay_runs, fast_rows


def each(start, stop, body):
    def step(i, carry):
        body(i)
        return carry

    lax.fori_loop(start, stop, step, 0)


def remote(src, dst, ssem, rsem, to):
    return pltpu.make_async_remote_copy(
        src_ref=src, dst_ref=dst, send_sem=ssem, recv_sem=rsem, device_id=(to,), device_id_type=MESH
    )


class Place:
    def __init__(self):
        self.me = me = lax.axis_index("dp")
        self.c, self.x, self.y, self.z = c, x, y, z = me % 2, (me // 2) % 2, (me // 4) % 2, me // 8
        self.lo = 1 - z // 2
        self.m = self.lo * z + (1 - self.lo) * (3 - z)
        sgn = 2 * self.lo - 1
        self.partner = self.dev(z, y, x, 1 - c)
        self.xn, self.yn = self.dev(z, y, 1 - x, c), self.dev(z, 1 - y, x, c)
        self.up = self.dev(z + sgn, y, x, c)
        self.down = self.dev(z - sgn, y, x, c)
        self.flat = me % 8
        self.zothers = [((z + d) % 4) * 8 + self.flat for d in (1, 2, 3)]
        self.plane = [z * 8 + (self.flat + d) % 8 for d in range(1, 8)]

    def dev(self, zz, yy, xx, cc):
        return ((zz * 2 + yy) * 2 + xx) * 2 + cc

    def pn(self, s):
        h = s % 2
        return self.xn * (1 - h) + self.yn * h

    def qn(self, s):
        h = s % 2
        return self.yn * (1 - h) + self.xn * h

    def chip(self, s, u, qo, po):
        h = s % 2
        first = self.x * (1 - h) + self.y * h
        last = self.y * (1 - h) + self.x * h
        pv = 1 - first if po else first
        qv = 1 - last if qo else last
        xx = pv * (1 - h) + qv * h
        yy = qv * (1 - h) + pv * h
        return ((self.lo * u + (1 - self.lo) * (3 - u)) * 2 + yy) * 2 + xx


def enter(others):
    barrier = pltpu.get_barrier_semaphore()
    for other in others:
        pl.semaphore_signal(barrier, inc=1, device_id=(other,), device_id_type=MESH)
    pl.semaphore_wait(barrier, len(others))


def reduce_kernel(
    lr_ref, grads, master, mom1, mom2,
    o_master, o_mom1, o_mom2, o_work, praw,
    stg, acc, zd, zu, fin, rb, nsum, nb, nr, nz,
    core_s, core_r, first_s, first_r, z_s, zd_r, zu_r, q_s, pre_r, fin_r, ld, st_ld, norm_s, norm_r,
):
    rows, width = acc.shape[2], acc.shape[3]
    shard = STREAMS * rows
    total_rows = grads.shape[1]
    tile = min(32, rows)
    at_dev = Place()
    me, c, m, chip, pn, qn = at_dev.me, at_dev.c, at_dev.m, at_dev.chip, at_dev.pn, at_dev.qn

    enter(at_dev.plane + at_dev.zothers)

    def grad_rows(ci, s, cc):
        return grads.at[0, pl.ds(pl.multiple_of((ci * 2 + cc) * shard + s * rows, rows), rows)]

    def praw_rows(ci, s):
        return praw.at[pl.ds(pl.multiple_of((ci * STREAMS + s) * rows, rows), rows)]

    def core_copy(ci, s):
        i = ci * STREAMS + s
        return remote(grad_rows(ci, s, 1 - c), praw_rows(ci, s), core_s.at[i], core_r.at[i], at_dev.partner)

    def each_of(group, body):
        each(group * GROUP, group * GROUP + GROUP, body)

    def loads(job, slot, s):
        kind, u, qo, group = job
        ci = chip(s, u, qo, kind == "first")
        i = s - group * GROUP
        own = pltpu.make_async_copy(grad_rows(ci, s, c), rb.at[slot, i, 0], ld.at[slot, i, 0])
        other = pltpu.make_async_copy(praw_rows(ci, s), rb.at[slot, i, 1], ld.at[slot, i, 1])
        return ci, own, other

    def swap(job):
        kind, u, qo, group = job
        each_of(group, lambda s: core_copy(chip(s, u, qo, kind == "first"), s).start())

    def prefetch(job, slot):
        def body(s):
            ci, own, other = loads(job, slot, s)
            core_copy(ci, s).wait_recv()
            own.start()
            other.start()

        each_of(job[3], body)

    def landed(ref, rsem):
        remote(ref, ref, core_s.at[0], rsem, me).wait_recv()

    def sent(ref, ssem):
        remote(ref, ref, ssem, core_r.at[0], me).wait_send()

    def run_job(job, slot, mid):
        kind, u, qo, group = job
        k = 2 * u + qo

        def body(s):
            _, own, other = loads(job, slot, s)
            parts = []
            if kind != "first":
                parts.append((acc.at[s, k], first_r.at[s, k]))
                if mid and u >= 1 and not (u == 3 and qo == 1):
                    parts.append((zd.at[s, k - 2], zd_r.at[s, k - 2]))
                if (mid and u <= 1) or (not mid and u == 0):
                    parts.append((zu.at[s, k], zu_r.at[s, k]))
                if not mid and (u, qo) == (3, 0):
                    parts.append((zd.at[s, 0], pre_r.at[s]))
                if kind == "res":
                    parts.append((fin.at[s], fin_r.at[s]))
            for ref, rsem in parts:
                landed(ref, rsem)
            own.wait()
            other.wait()
            dst = stg.at[s, k] if kind == "first" else acc.at[s, k]
            i = s - group * GROUP

            def add(t):
                at = pl.ds(pl.multiple_of(t * tile, tile), tile)
                v = rb[slot, i, 0, at, :].astype(jnp.float32) + rb[slot, i, 1, at, :].astype(jnp.float32)
                for ref, _ in parts:
                    v = v + ref[at, :]
                if kind == "res":
                    v = v * (1.0 / 32.0)
                    nsum[...] += jnp.sum((v * v).reshape(tile // 8, 8, width), axis=0)
                dst[at, :] = v

            each(0, rows // tile, add)
            if kind == "first":
                remote(dst, acc.at[s, k], first_s.at[s, k], first_r.at[s, k], pn(s)).start()
            elif kind == "pre":
                remote(dst, zd.at[s, 0], q_s.at[s, 0], pre_r.at[s], qn(s)).start()
            elif kind == "fin":
                remote(dst, fin.at[s], q_s.at[s, 1], fin_r.at[s], qn(s)).start()
            elif kind == "up" and not mid:
                remote(dst, zd.at[s, k - 2], z_s.at[s, k], zd_r.at[s, k - 2], at_dev.up).start()
            elif kind == "up":
                kk = 2 * (3 - u) + qo
                remote(dst, zu.at[s, kk], z_s.at[s, k], zu_r.at[s, kk], at_dev.up).start()
            elif kind == "down":
                remote(dst, zu.at[s, k], z_s.at[s, k], zu_r.at[s, k], at_dev.down).start()

        each_of(group, body)

    def state_load(s):
        at = pl.ds(pl.multiple_of(s * rows, rows), rows)
        return [
            pltpu.make_async_copy(src.at[at], dst.at[at], st_ld.at[i, s])
            for i, (src, dst) in enumerate(((master, o_master), (mom1, o_mom1), (mom2, o_mom2)))
        ]

    def start_state(s):
        for copy in state_load(s):
            copy.start()

    def reduce_program(jobs, mid):
        ahead = 3
        for job in jobs[:ahead]:
            swap(job)
        prefetch(jobs[0], 0)
        for j, job in enumerate(jobs):
            if j + ahead < len(jobs):
                swap(jobs[j + ahead])
            if j + 1 < len(jobs):
                prefetch(jobs[j + 1], (j + 1) % 2)
            run_job(job, j % 2, mid)
            if j == 16:
                each(0, STREAMS, start_state)

    nsum[...] = jnp.zeros_like(nsum)

    @pl.when(m == 0)
    def _():
        reduce_program(END_JOBS, False)

    @pl.when(m == 1)
    def _():
        reduce_program(MID_JOBS, True)

    def all_sum(part, place, count, others, slots, src, base):
        src[...] = part
        slots[place] = part
        for i, (other, _) in enumerate(others):
            remote(src, slots.at[place], norm_s.at[base + i], norm_r.at[base + place], other).start()
        for i, (_, slot) in enumerate(others):
            landed(slots.at[slot], norm_r.at[base + slot])
        total = slots[0]
        for i in range(1, count):
            total = total + slots[i]
        return total

    part = nsum[:, 0:128]
    for col in range(128, width, 128):
        part = part + nsum[:, col:col + 128]
    flat, z = at_dev.flat, at_dev.z
    part = all_sum(part, flat, 8, [(d, (flat + i + 1) % 8) for i, d in enumerate(at_dev.plane)], nr, nb.at[0], 0)
    part = all_sum(part, z, 4, [(d, (z + i + 1) % 4) for i, d in enumerate(at_dev.zothers)], nz, nb.at[1], 8)
    square_sum = jnp.sum(part, keepdims=True)
    clip = jnp.minimum(1.0, 1.0 / (jnp.sqrt(square_sum) + 1e-6))
    clip = jnp.broadcast_to(clip, (tile, 128))

    learn_rate = lr_ref[0]
    inv1 = 1.0 / (1.0 - 0.9 ** ADAM_STEP)
    inv2 = 1.0 / (1.0 - 0.99 ** ADAM_STEP)
    decay_runs, fast_rows = rule_runs(width, total_rows)

    def update(s):
        for copy in state_load(s):
            copy.wait()

        def rows_step(t):
            base = pl.multiple_of(t * tile, tile)
            at = pl.ds(base, tile)
            out_at = pl.ds(pl.multiple_of(s * rows + t * tile, tile), tile)
            row = me * shard + s * rows + base + lax.broadcasted_iota(jnp.int32, (tile, 128), 0)
            decays = (row >= decay_runs[0][0]) & (row < decay_runs[0][1])
            for start, stop in decay_runs[1:]:
                decays = decays | ((row >= start) & (row < stop))
            fast = row == fast_rows[0]
            for fast_row in fast_rows[1:]:
                fast = fast | (row == fast_row)
            decay = jnp.where(decays, 0.1, 0.0)
            step_size = learn_rate * jnp.where(fast, 2.0, 1.0)
            for col in range(0, width, 128):
                cols = pl.ds(col, 128)
                g = acc[s, 2 * m, at, cols] * clip
                old = o_master[out_at, cols]
                first = 0.9 * o_mom1[out_at, cols] + 0.1 * g
                second = 0.99 * o_mom2[out_at, cols] + 0.01 * (g * g)
                new = old - step_size * ((first * inv1) / (jnp.sqrt(second * inv2) + 1e-8) + decay * old)
                o_master[out_at, cols] = new
                o_mom1[out_at, cols] = first
                o_mom2[out_at, cols] = second
                o_work[out_at, cols] = new.astype(jnp.bfloat16)

        each(0, rows // tile, rows_step)

    each(0, STREAMS, update)

    block = acc.at[0, 0]

    def drain(jobs):
        for kind, u, qo, group in jobs:
            k = 2 * u + qo
            if kind == "first":
                each_of(group, lambda s: sent(block, first_s.at[s, k]))
            elif kind in ("up", "down"):
                each_of(group, lambda s: sent(block, z_s.at[s, k]))

    @pl.when(m == 0)
    def _():
        drain([j for j in END_JOBS if j[0] != "first"])
        each(0, STREAMS, lambda s: sent(block, q_s.at[s, 0]))

    @pl.when(m == 1)
    def _():
        drain([j for j in MID_JOBS if j[0] != "first"])

    each(0, 8 * STREAMS, lambda i: sent(block, first_s.at[i // 8, i % 8]))
    each(0, STREAMS, lambda s: sent(block, q_s.at[s, 1]))
    each(0, 16 * STREAMS, lambda i: core_copy(i // STREAMS, i % STREAMS).wait_send())
    for i in range(7):
        sent(nb.at[0], norm_s.at[i])
    for i in range(3):
        sent(nb.at[1], norm_s.at[8 + i])


def gather_kernel(own_ref, o_work, own_s, gat_r, gcore_r, gcore_s, gp_s, gu_s, gd_s, gq_s):
    shard, width = own_ref.shape
    rows = shard // STREAMS
    at_dev = Place()
    me, c, m, chip = at_dev.me, at_dev.c, at_dev.m, at_dev.chip
    my_chip = me // 2

    enter([at_dev.partner, at_dev.xn, at_dev.yn] + at_dev.zothers)

    def work_rows(ci, s, cc):
        return o_work.at[pl.ds(pl.multiple_of((ci * 2 + cc) * shard + s * rows, rows), rows)]

    def send(src, ci, s, k, link):
        dst = work_rows(ci, s, c)
        i = ci * STREAMS + s
        if link == "c":
            remote(src, dst, gcore_s.at[i], gcore_r.at[i], at_dev.partner).start()
        else:
            to = {"p": at_dev.pn(s), "q": at_dev.qn(s), "u": at_dev.up, "d": at_dev.down}[link]
            ssem = {"p": gp_s, "q": gq_s, "u": gu_s, "d": gd_s}[link]
            remote(src, dst, ssem.at[s, k], gat_r.at[i], to).start()

    def gather_program(sends, own):
        first = [t for t in sends if t[:3] == own and t[4] == 0]

        def start_own(s):
            src = own_ref.at[pl.ds(pl.multiple_of(s * rows, rows), rows)]
            for u, qo, _, link, _ in first:
                send(src, my_chip, s, 2 * u + qo, link)

        each(0, STREAMS, start_own)

        def keep(t):
            at = pl.multiple_of(t * 32, 32)
            o_work[pl.ds(pl.multiple_of(me * shard + at, 32), 32), :] = own_ref[pl.ds(at, 32), :]

        each(0, shard // 32, keep)
        rest = [t for t in sends if t[:3] != own]
        seen = set()
        n = 0
        while n < len(rest):
            block, group = rest[n][:3], rest[n][4]
            links = [rest[n][3]]
            while n + 1 < len(rest) and rest[n + 1][:3] == block and rest[n + 1][4] == group:
                n += 1
                links.append(rest[n][3])
            n += 1
            new = (block, group) not in seen
            seen.add((block, group))

            def body(s, block=block, links=tuple(links), new=new):
                ci = chip(s, *block)
                ref = work_rows(ci, s, c)
                if new:
                    remote(ref, ref, gcore_s.at[0], gat_r.at[ci * STREAMS + s], me).wait_recv()
                for link in links:
                    send(ref, ci, s, 2 * block[0] + block[1], link)

            each(group * GROUP, group * GROUP + GROUP, body)
        block_ref = own_ref.at[pl.ds(0, rows)]
        for link, ssem in (("p", gp_s), ("q", gq_s), ("u", gu_s), ("d", gd_s)):
            for k in sorted({2 * t[0] + t[1] for t in sends if t[3] == link}):
                each(0, STREAMS, lambda s: remote(block_ref, block_ref, ssem.at[s, k], gat_r.at[0], me).wait_send())

    @pl.when(m == 0)
    def _():
        gather_program(END_SENDS, (0, 0, 0))

    @pl.when(m == 1)
    def _():
        gather_program(MID_SENDS, (1, 0, 0))

    def drain_core(i):
        ci, s = i // STREAMS, i % STREAMS
        ref = work_rows(ci, s, 1 - c)
        remote(ref, ref, gcore_s.at[i], gcore_r.at[i], me).wait()

    each(0, 16 * STREAMS, drain_core)


def store_kernel(*refs):
    ins, outs, sem = refs[:4], refs[4:8], refs[8]
    copies = [pltpu.make_async_copy(src, dst, sem.at[i]) for i, (src, dst) in enumerate(zip(ins[:3], outs[:3]))]
    pieces = sem.shape[0] - 3
    rows = ins[3].shape[0] // pieces
    for i in range(pieces):
        at = pl.ds(i * rows, rows)
        copies.append(pltpu.make_async_copy(ins[3].at[at], outs[3].at[at], sem.at[3 + i]))
    for copy in copies:
        copy.start()
    for copy in copies:
        copy.wait()


def solution(mesh):
    dev_count = mesh.shape["dp"]

    def device_step(local_grads, master, mom_first, mom_second, learn_rate):
        shard_rows, width = master.shape
        total_rows = shard_rows * dev_count
        rows = shard_rows // STREAMS
        any_spec = pl.BlockSpec(memory_space=pl.ANY)
        vmem_spec = pl.BlockSpec(memory_space=pltpu.VMEM)
        dma = pltpu.SemaphoreType.DMA
        f32, bf16 = jnp.float32, jnp.bfloat16
        shard = pltpu.VMEM((shard_rows, width), f32)
        new_master, new_first, new_second, own_rows, _ = pl.pallas_call(
            reduce_kernel,
            out_shape=[
                shard, shard, shard,
                pltpu.VMEM((shard_rows, width), bf16),
                jax.ShapeDtypeStruct((total_rows // 2, width), bf16),
            ],
            in_specs=[pl.BlockSpec(memory_space=pltpu.SMEM)] + [any_spec] * 4,
            out_specs=[vmem_spec] * 4 + [any_spec],
            scratch_shapes=[
                pltpu.VMEM((STREAMS, 8, rows, width), f32),
                pltpu.VMEM((STREAMS, 8, rows, width), f32),
                pltpu.VMEM((STREAMS, 5, rows, width), f32),
                pltpu.VMEM((STREAMS, 4, rows, width), f32),
                pltpu.VMEM((STREAMS, rows, width), f32),
                pltpu.VMEM((2, GROUP, 2, rows, width), bf16),
                pltpu.VMEM((8, width), f32),
                pltpu.VMEM((2, 8, 128), f32),
                pltpu.VMEM((8, 8, 128), f32),
                pltpu.VMEM((4, 8, 128), f32),
                dma((16 * STREAMS,)), dma((16 * STREAMS,)),
                dma((STREAMS, 8)), dma((STREAMS, 8)),
                dma((STREAMS, 8)), dma((STREAMS, 5)), dma((STREAMS, 4)),
                dma((STREAMS, 2)), dma((STREAMS,)), dma((STREAMS,)),
                dma((2, GROUP, 2)), dma((3, STREAMS)),
                dma((12,)), dma((12,)),
            ],
            compiler_params=pltpu.CompilerParams(
                collective_id=0, has_side_effects=True, vmem_limit_bytes=56 * 2 ** 20
            ),
            name="reduce_update",
        )(learn_rate.reshape(1), local_grads, master, mom_first, mom_second)
        working = pl.pallas_call(
            gather_kernel,
            out_shape=pltpu.VMEM((total_rows, width), bf16),
            in_specs=[vmem_spec],
            out_specs=vmem_spec,
            scratch_shapes=[
                dma((STREAMS,)), dma((16 * STREAMS,)), dma((16 * STREAMS,)), dma((16 * STREAMS,)),
                dma((STREAMS, 8)), dma((STREAMS, 8)), dma((STREAMS, 8)), dma((STREAMS, 8)),
            ],
            compiler_params=pltpu.CompilerParams(
                collective_id=1, has_side_effects=True, vmem_limit_bytes=4 * 2 ** 20
            ),
            name="gather_rows",
        )(own_rows)
        return pl.pallas_call(
            store_kernel,
            out_shape=[jax.ShapeDtypeStruct((shard_rows, width), f32)] * 3
            + [jax.ShapeDtypeStruct((total_rows, width), bf16)],
            in_specs=[vmem_spec] * 4,
            out_specs=[any_spec] * 4,
            scratch_shapes=[dma((3 + 8,))],
            compiler_params=pltpu.CompilerParams(vmem_limit_bytes=4 * 2 ** 20),
            name="store",
        )(new_master, new_first, new_second, working)

    return jax.shard_map(
        device_step,
        mesh=mesh,
        in_specs=(P("dp", None, None), P("dp", None), P("dp", None), P("dp", None), P()),
        out_specs=(P("dp", None), P("dp", None), P("dp", None), P(None, None)),
        check_vma=False,
    )
```

time: 1030 us -> 401 us (0.39)
  waiting for transfers between devices: 898 us -> 0 us
  Pallas kernels: 0 us -> 399 us
  blocking collectives: 47.1 us -> 0 us
  other arithmetic: 41.5 us -> 0 us
  local copies, waits for them, and re-layouts: 23.2 us -> 0 us
  between operations: 15.5 us -> 1.29 us
    reduce_scatter x1 -> x0, waiting for transfers between devices: 705 us -> none  [device_step(): lax.psum_scatter(local_grads[0].astype(jnp.float32), 'dp', scatter_dimens...]
    pallas_call x0 -> x3, Pallas kernels: none -> 399 us  [the longest x1 260 us: device_step(): pl.pallas_call(reduce_kernel, out_shape=[shard, shard, shard, pltpu.VMEM(...]
    all_gather x1 -> x0, waiting for transfers between devices: 194 us -> none  [device_step(): lax.all_gather(new_master.astype(jnp.bfloat16), 'dp', axis=0, tiled=True)]
    psum x1 -> x0, blocking collectives: 47.1 us -> none  [device_step(): square_sum = lax.psum(jnp.sum(grad_shard * grad_shard), 'dp')]
    convert_element_type x2 -> x0, other arithmetic: 38.4 us -> none  [the longest x1 32.4 us: device_step(): local_grads[0].astype(jnp.float32)]
    unnamed x5 -> x0, local copies, waits for them, and re-layouts: 23.2 us -> none
  transfers between devices with their start and end apart: 2 -> 0, of which waited for: 2 -> 0; matrix products, arithmetic and copies ran while one was open for 0% -> 0% of each run, Pallas kernels for 0% -> 0%
where the time goes in v2:
time: 401 us; the launch traced here: 400 us
  Pallas kernels  399 us (100%)
    pallas_call x1, Pallas kernels, device_step(): pl.pallas_call(reduce_kernel, out_shape=[shard, shard, shard, pltpu.VMEM(...  260 us
    pallas_call x1, Pallas kernels, device_step(): pl.pallas_call(gather_kernel, out_shape=pltpu.VMEM((total_rows, width), b...  126 us
    pallas_call x1, Pallas kernels, device_step(): pl.pallas_call(store_kernel, out_shape=[jax.ShapeDtypeStruct((shard_rows,...  13 us

profile of v2, /device:TPU:0, one launch (start us, length us, event | category | flops | bytes accessed | tf_op | source)
XLA Modules:
  0.0 400.3 jit_solution(17750569314600423264)
XLA Ops:
  1.3 259.9 %reduce_update.1 = (f32[1024,512]{1,0:T(8,128)S(1)}, f32[1024,512]{1,0:T(8,128)S(1)}, f32[1024,512]{1,0:T(8,128)S(1)}, bf16[1024,512]{1,0:T(8,128)(2,1)S(1)}, bf16[16384,512]{1,0:T(8,128)(2,1)}) custom-call(f32[1]{0:T(128)} %bitcast.1.lr_ref, bf16[1,32768,512]{2,1,0:T(8,128)(2,1)} %grads.1, f32[1024,512]{1,0:T(8,128)} %master.1, f32[1024,512]{1,0:T(8,128)} %mom1.1, ...), custom_call_target="tpu_custom_call" | custom-call | tf_op jit(solution)/shard_map/reduce_update/pallas_call | solution.py:481
  261.2 126.1 %gather_rows.1.refs_3_ = bf16[32768,512]{1,0:T(8,128)(2,1)S(1)} custom-call(bf16[1024,512]{1,0:T(8,128)(2,1)S(1)} %get-tuple-element.11.own_ref), custom_call_target="tpu_custom_call" | custom-call | tf_op jit(solution)/shard_map/gather_rows/pallas_call | solution.py:513
  387.3 13.0 %store.1 = (f32[1024,512]{1,0:T(8,128)}, f32[1024,512]{1,0:T(8,128)}, f32[1024,512]{1,0:T(8,128)}, bf16[32768,512]{1,0:T(8,128)(2,1)}) custom-call(f32[1024,512]{1,0:T(8,128)S(1)} %get-tuple-element.8.refs_0_, f32[1024,512]{1,0:T(8,128)S(1)} %get-tuple-element.9.refs_1_, f32[1024,512]{1,0:T(8,128)S(1)} %get-tuple-element.10.refs_2_, ...), custom_call_target="tpu_custom_call" | custom-call | tf_op jit(solution)/shard_map/store/pallas_call | solution.py:527

commit v3 on v2

--- a/solution.py
+++ b/solution.py
@@ -9,58 +9,41 @@
 MIX_RANK = 32
 DECAY_RANK = 64
 ADAM_STEP = 10
-STREAMS = 8
-GROUP = 4
+STREAMS = 16
+GROUP = 8
+LAG = 20
 MESH = pl.DeviceIdType.MESH
 
-END_JOBS = [
-    ("first", 2, 0, 1), ("first", 2, 1, 1), ("first", 2, 0, 0), ("first", 3, 1, 1), ("up", 2, 0, 1),
-    ("up", 2, 1, 1), ("first", 1, 1, 1), ("first", 1, 0, 0), ("up", 1, 1, 1), ("first", 2, 1, 0),
-    ("first", 3, 1, 0), ("up", 2, 1, 0), ("pre", 3, 1, 0), ("first", 1, 1, 0), ("first", 3, 0, 0),
-    ("up", 2, 0, 0), ("up", 1, 1, 0), ("pre", 3, 1, 1), ("first", 0, 1, 0), ("first", 3, 0, 1),
-    ("first", 0, 1, 1), ("up", 3, 0, 0), ("up", 3, 0, 1), ("first", 1, 0, 1), ("fin", 0, 1, 1),
-    ("fin", 0, 1, 0), ("up", 1, 0, 0), ("first", 0, 0, 0), ("first", 0, 0, 1), ("up", 1, 0, 1),
-    ("res", 0, 0, 0), ("res", 0, 0, 1),
-]
-MID_JOBS = [
-    ("first", 3, 1, 0), ("first", 3, 1, 1), ("first", 2, 0, 1), ("first", 1, 0, 1), ("up", 2, 0, 1),
-    ("up", 3, 1, 1), ("first", 2, 1, 0), ("first", 2, 1, 1), ("first", 0, 1, 0), ("first", 1, 1, 0),
-    ("first", 3, 0, 1), ("first", 0, 1, 1), ("up", 3, 1, 0), ("first", 3, 0, 0), ("up", 2, 1, 0),
-    ("first", 1, 1, 1), ("up", 2, 1, 1), ("first", 0, 0, 0), ("first", 0, 0, 1), ("down", 0, 1, 0),
-    ("first", 2, 0, 0), ("down", 0, 1, 1), ("up", 3, 0, 0), ("down", 0, 0, 0), ("up", 3, 0, 1),
-    ("fin", 1, 1, 0), ("first", 1, 0, 0), ("fin", 1, 1, 1), ("down", 0, 0, 1), ("up", 2, 0, 0),
-    ("res", 1, 0, 0), ("res", 1, 0, 1),
-]
-END_SENDS = [
-    (0, 0, 0, "q", 0), (0, 0, 0, "q", 1), (0, 0, 0, "u", 0), (0, 0, 0, "u", 1), (0, 0, 0, "p", 0),
-    (0, 0, 0, "p", 1), (0, 0, 0, "c", 0), (0, 0, 0, "c", 1), (1, 0, 0, "p", 1), (0, 1, 0, "u", 0),
-    (0, 0, 1, "c", 1), (0, 1, 0, "u", 1), (0, 1, 0, "p", 1), (1, 0, 0, "p", 0), (3, 0, 0, "p", 0),
-    (1, 0, 0, "c", 1), (3, 0, 0, "c", 0), (0, 1, 0, "p", 0), (3, 0, 0, "q", 0), (3, 0, 0, "q", 1),
-    (2, 0, 0, "c", 0), (3, 1, 0, "c", 0), (2, 0, 0, "p", 0), (3, 0, 0, "c", 1), (0, 1, 0, "c", 1),
-    (0, 1, 1, "c", 0), (3, 0, 0, "p", 1), (2, 0, 0, "p", 1), (0, 1, 0, "c", 0), (3, 1, 0, "p", 0),
-    (3, 0, 1, "c", 0), (2, 1, 0, "p", 0), (2, 0, 1, "c", 1), (3, 0, 1, "c", 1), (2, 0, 0, "c", 1),
-    (3, 1, 0, "c", 1), (1, 1, 0, "p", 1), (3, 1, 0, "p", 1), (0, 0, 1, "c", 0), (2, 1, 0, "p", 1),
-    (1, 1, 0, "c", 1), (2, 1, 0, "c", 0), (1, 1, 1, "c", 1), (0, 1, 1, "c", 1), (1, 0, 1, "c", 1),
-    (2, 0, 1, "c", 0), (2, 1, 0, "c", 1), (3, 1, 1, "c", 1), (2, 1, 1, "c", 0), (3, 1, 1, "c", 0),
-    (1, 0, 0, "c", 0), (1, 1, 0, "p", 0), (2, 1, 1, "c", 1), (1, 1, 0, "c", 0), (1, 0, 1, "c", 0),
-    (1, 1, 1, "c", 0),
-]
-MID_SENDS = [
-    (1, 0, 0, "q", 0), (1, 0, 0, "q", 1), (1, 0, 0, "u", 0), (1, 0, 0, "u", 1), (1, 0, 0, "d", 0),
-    (1, 0, 0, "d", 1), (1, 0, 0, "p", 0), (1, 0, 0, "p", 1), (1, 0, 0, "c", 0), (1, 0, 0, "c", 1),
-    (2, 0, 0, "d", 0), (0, 0, 0, "u", 0), (0, 0, 0, "p", 1), (2, 0, 0, "c", 1), (2, 0, 0, "p", 1),
-    (2, 0, 0, "p", 0), (0, 0, 0, "u", 1), (3, 0, 0, "d", 0), (1, 1, 0, "u", 0), (0, 1, 0, "p", 0),
-    (1, 1, 0, "u", 1), (1, 1, 0, "p", 1), (3, 0, 0, "p", 0), (3, 0, 0, "d", 1), (0, 1, 0, "p", 1),
-    (2, 0, 0, "c", 0), (2, 0, 0, "d", 1), (1, 1, 0, "d", 1), (0, 1, 0, "u", 1), (2, 1, 0, "d", 0),
-    (0, 1, 0, "c", 0), (0, 1, 0, "u", 0), (0, 0, 0, "p", 0), (2, 0, 1, "c", 0), (3, 0, 1, "c", 0),
-    (2, 1, 0, "p", 1), (1, 1, 0, "p", 0), (0, 0, 0, "c", 0), (2, 1, 0, "d", 1), (2, 1, 1, "c", 1),
-    (1, 1, 0, "c", 0), (2, 0, 1, "c", 1), (2, 1, 0, "p", 0), (3, 1, 0, "p", 1), (1, 1, 1, "c", 0),
-    (3, 0, 0, "c", 1), (0, 1, 1, "c", 1), (1, 1, 0, "c", 1), (2, 1, 0, "c", 1), (0, 1, 1, "c", 0),
-    (1, 1, 0, "d", 0), (3, 1, 0, "c", 1), (0, 0, 1, "c", 1), (3, 1, 0, "p", 0), (3, 0, 0, "p", 1),
-    (0, 0, 0, "c", 1), (0, 0, 1, "c", 0), (2, 1, 0, "c", 0), (1, 1, 1, "c", 1), (3, 1, 1, "c", 1),
-    (1, 0, 1, "c", 1), (0, 1, 0, "c", 1), (2, 1, 1, "c", 0), (3, 0, 0, "c", 0), (1, 0, 1, "c", 0),
-    (3, 1, 0, "c", 0), (3, 1, 1, "c", 0), (3, 0, 1, "c", 1),
-]
+
+def decode(codes):
+    return [tuple(int(ch) if ch.isdigit() else ch for ch in code) for code in codes]
+
+
+END_JOBS = decode([
+    "f210", "f201", "u210", "f211", "f200", "f301", "u211", "f110", "u200", "f310", "u110", "u201",
+    "f300", "f311", "p310", "f011", "f100", "f111", "u300", "p311", "f101", "u111", "u301", "n011",
+    "u100", "f010", "f000", "n010", "f001", "u101", "r000", "r001",
+])
+MID_JOBS = decode([
+    "f211", "f311", "f310", "u311", "f010", "f011", "u310", "f300", "d011", "f200", "f210", "f101",
+    "f201", "u200", "u211", "d010", "f301", "f100", "u210", "f111", "f110", "f000", "f001", "u300",
+    "n110", "u201", "d000", "n111", "u301", "d001", "r100", "r101",
+])
+END_SENDS = decode([
+    "000q0", "000q1", "000u0", "000u1", "000p0", "000p1", "000c0", "000c1", "100p0", "100c1", "010u1", "010p0",
+    "200p1", "010c0", "010p1", "300p0", "300q0", "010u0", "310p0", "100p1", "201c1", "300p1", "300q1", "200p0",
+    "011c0", "001c1", "310p1", "300c1", "310c1", "100c0", "210p1", "210c1", "301c0", "301c1", "300c0", "110p1",
+    "101c1", "200c0", "200c1", "110c1", "101c0", "201c0", "001c0", "010c1", "110p0", "211c1", "110c0", "311c0",
+    "311c1", "111c1", "111c0", "310c0", "210p0", "210c0", "011c1", "211c0",
+])
+MID_SENDS = decode([
+    "100q0", "100q1", "100u0", "100u1", "100d0", "100d1", "100p0", "100p1", "100c0", "100c1", "200p0", "000p0",
+    "200d1", "000p1", "000u0", "000u1", "110u1", "101c0", "200c0", "300d0", "200d0", "200p1", "010c1", "110p1",
+    "110c1", "300p0", "300d1", "110d1", "300p1", "111c1", "201c1", "110u0", "010u0", "210d1", "110p0", "301c1",
+    "010c0", "000c1", "201c0", "001c0", "010u1", "210p1", "300c0", "210c0", "010p1", "010p0", "310c0", "110d0",
+    "111c0", "310p0", "210c1", "210p0", "300c1", "310p1", "301c0", "200c1", "101c1", "011c1", "311c0", "211c1",
+    "011c0", "210d0", "310c1", "000c0", "311c1", "211c0", "110c0", "001c1",
+])
 
 
 def rule_runs(model_width, total_rows):
@@ -164,31 +147,33 @@
     def praw_rows(ci, s):
         return praw.at[pl.ds(pl.multiple_of((ci * STREAMS + s) * rows, rows), rows)]
 
-    def core_copy(ci, s):
+    def core_copy(ci, s, dst=None):
         i = ci * STREAMS + s
-        return remote(grad_rows(ci, s, 1 - c), praw_rows(ci, s), core_s.at[i], core_r.at[i], at_dev.partner)
+        dst = praw_rows(ci, s) if dst is None else dst
+        return remote(grad_rows(ci, s, 1 - c), dst, core_s.at[i], core_r.at[i], at_dev.partner)
 
     def each_of(group, body):
         each(group * GROUP, group * GROUP + GROUP, body)
 
-    def loads(job, slot, s):
+    def loads(job, j, s):
         kind, u, qo, group = job
-        ci = chip(s, u, qo, kind == "first")
-        i = s - group * GROUP
+        ci = chip(s, u, qo, kind == "f")
+        slot, i = j % 2, s - group * GROUP
         own = pltpu.make_async_copy(grad_rows(ci, s, c), rb.at[slot, i, 0], ld.at[slot, i, 0])
-        other = pltpu.make_async_copy(praw_rows(ci, s), rb.at[slot, i, 1], ld.at[slot, i, 1])
-        return ci, own, other
-
-    def swap(job):
-        kind, u, qo, group = job
-        each_of(group, lambda s: core_copy(chip(s, u, qo, kind == "first"), s).start())
-
-    def prefetch(job, slot):
+        if j < 2:
+            return own, core_copy(ci, s, rb.at[slot, i, 1]), None
+        return own, core_copy(ci, s), pltpu.make_async_copy(praw_rows(ci, s), rb.at[slot, i, 1], ld.at[slot, i, 1])
+
+    def swap(job, j):
+        each_of(job[3], lambda s: loads(job, j, s)[1].start())
+
+    def prefetch(job, j):
         def body(s):
-            ci, own, other = loads(job, slot, s)
-            core_copy(ci, s).wait_recv()
+            own, core, other = loads(job, j, s)
             own.start()
-            other.start()
+            if other is not None:
+                core.wait_recv()
+                other.start()
 
         each_of(job[3], body)
 
@@ -198,14 +183,15 @@
     def sent(ref, ssem):
         remote(ref, ref, ssem, core_r.at[0], me).wait_send()
 
-    def run_job(job, slot, mid):
+    def run_job(job, j, mid):
         kind, u, qo, group = job
         k = 2 * u + qo
+        slot = j % 2
 
         def body(s):
-            _, own, other = loads(job, slot, s)
+            own, core, other = loads(job, j, s)
             parts = []
-            if kind != "first":
+            if kind != "f":
                 parts.append((acc.at[s, k], first_r.at[s, k]))
                 if mid and u >= 1 and not (u == 3 and qo == 1):
                     parts.append((zd.at[s, k - 2], zd_r.at[s, k - 2]))
@@ -213,13 +199,16 @@
                     parts.append((zu.at[s, k], zu_r.at[s, k]))
                 if not mid and (u, qo) == (3, 0):
                     parts.append((zd.at[s, 0], pre_r.at[s]))
-                if kind == "res":
+                if kind == "r":
                     parts.append((fin.at[s], fin_r.at[s]))
             for ref, rsem in parts:
                 landed(ref, rsem)
             own.wait()
-            other.wait()
-            dst = stg.at[s, k] if kind == "first" else acc.at[s, k]
+            if other is None:
+                core.wait_recv()
+            else:
+                other.wait()
+            dst = stg.at[s, k] if kind == "f" else acc.at[s, k]
             i = s - group * GROUP
 
             def add(t):
@@ -227,24 +216,24 @@
                 v = rb[slot, i, 0, at, :].astype(jnp.float32) + rb[slot, i, 1, at, :].astype(jnp.float32)
                 for ref, _ in parts:
                     v = v + ref[at, :]
-                if kind == "res":
+                if kind == "r":
                     v = v * (1.0 / 32.0)
                     nsum[...] += jnp.sum((v * v).reshape(tile // 8, 8, width), axis=0)
                 dst[at, :] = v
 
             each(0, rows // tile, add)
-            if kind == "first":
+            if kind == "f":
                 remote(dst, acc.at[s, k], first_s.at[s, k], first_r.at[s, k], pn(s)).start()
-            elif kind == "pre":
+            elif kind == "p":
                 remote(dst, zd.at[s, 0], q_s.at[s, 0], pre_r.at[s], qn(s)).start()
-            elif kind == "fin":
+            elif kind == "n":
                 remote(dst, fin.at[s], q_s.at[s, 1], fin_r.at[s], qn(s)).start()
-            elif kind == "up" and not mid:
+            elif kind == "u" and not mid:
                 remote(dst, zd.at[s, k - 2], z_s.at[s, k], zd_r.at[s, k - 2], at_dev.up).start()
-            elif kind == "up":
+            elif kind == "u":
                 kk = 2 * (3 - u) + qo
                 remote(dst, zu.at[s, kk], z_s.at[s, k], zu_r.at[s, kk], at_dev.up).start()
-            elif kind == "down":
+            elif kind == "d":
                 remote(dst, zu.at[s, k], z_s.at[s, k], zu_r.at[s, k], at_dev.down).start()
 
         each_of(group, body)
@@ -262,16 +251,16 @@
 
     def reduce_program(jobs, mid):
         ahead = 3
-        for job in jobs[:ahead]:
-            swap(job)
+        for j in range(ahead):
+            swap(jobs[j], j)
         prefetch(jobs[0], 0)
         for j, job in enumerate(jobs):
             if j + ahead < len(jobs):
-                swap(jobs[j + ahead])
+                swap(jobs[j + ahead], j + ahead)
             if j + 1 < len(jobs):
-                prefetch(jobs[j + 1], (j + 1) % 2)
-            run_job(job, j % 2, mid)
-            if j == 16:
+                prefetch(jobs[j + 1], j + 1)
+            run_job(job, j, mid)
+            if j == len(jobs) // 2:
                 each(0, STREAMS, start_state)
 
     nsum[...] = jnp.zeros_like(nsum)
@@ -284,11 +273,33 @@
     def _():
         reduce_program(MID_JOBS, True)
 
-    def all_sum(part, place, count, others, slots, src, base):
+    def drain():
+        block = acc.at[0, 0]
+
+        @pl.when(m == 0)
+        def _():
+            for kind, u, qo, group in END_JOBS:
+                if kind == "u":
+                    each_of(group, lambda s: sent(block, z_s.at[s, 2 * u + qo]))
+            each(0, STREAMS, lambda s: sent(block, q_s.at[s, 0]))
+
+        @pl.when(m == 1)
+        def _():
+            for kind, u, qo, group in MID_JOBS:
+                if kind == "u" or kind == "d":
+                    each_of(group, lambda s: sent(block, z_s.at[s, 2 * u + qo]))
+
+        each(0, 8 * STREAMS, lambda i: sent(block, first_s.at[i // 8, i % 8]))
+        each(0, STREAMS, lambda s: sent(block, q_s.at[s, 1]))
+        each(0, 16 * STREAMS, lambda i: core_copy(i // STREAMS, i % STREAMS).wait_send())
+
+    def all_sum(part, place, count, others, slots, src, base, meanwhile=None):
         src[...] = part
         slots[place] = part
         for i, (other, _) in enumerate(others):
             remote(src, slots.at[place], norm_s.at[base + i], norm_r.at[base + place], other).start()
+        if meanwhile is not None:
+            meanwhile()
         for i, (_, slot) in enumerate(others):
             landed(slots.at[slot], norm_r.at[base + slot])
         total = slots[0]
@@ -300,7 +311,7 @@
     for col in range(128, width, 128):
         part = part + nsum[:, col:col + 128]
     flat, z = at_dev.flat, at_dev.z
-    part = all_sum(part, flat, 8, [(d, (flat + i + 1) % 8) for i, d in enumerate(at_dev.plane)], nr, nb.at[0], 0)
+    part = all_sum(part, flat, 8, [(d, (flat + i + 1) % 8) for i, d in enumerate(at_dev.plane)], nr, nb.at[0], 0, drain)
     part = all_sum(part, z, 4, [(d, (z + i + 1) % 4) for i, d in enumerate(at_dev.zothers)], nz, nb.at[1], 8)
     square_sum = jnp.sum(part, keepdims=True)
     clip = jnp.minimum(1.0, 1.0 / (jnp.sqrt(square_sum) + 1e-6))
@@ -344,28 +355,6 @@
 
     each(0, STREAMS, update)
 
-    block = acc.at[0, 0]
-
-    def drain(jobs):
-        for kind, u, qo, group in jobs:
-            k = 2 * u + qo
-            if kind == "first":
-                each_of(group, lambda s: sent(block, first_s.at[s, k]))
-            elif kind in ("up", "down"):
-                each_of(group, lambda s: sent(block, z_s.at[s, k]))
-
-    @pl.when(m == 0)
-    def _():
-        drain([j for j in END_JOBS if j[0] != "first"])
-        each(0, STREAMS, lambda s: sent(block, q_s.at[s, 0]))
-
-    @pl.when(m == 1)
-    def _():
-        drain([j for j in MID_JOBS if j[0] != "first"])
-
-    each(0, 8 * STREAMS, lambda i: sent(block, first_s.at[i // 8, i % 8]))
-    each(0, STREAMS, lambda s: sent(block, q_s.at[s, 1]))
-    each(0, 16 * STREAMS, lambda i: core_copy(i // STREAMS, i % STREAMS).wait_send())
     for i in range(7):
         sent(nb.at[0], norm_s.at[i])
     for i in range(3):
@@ -409,18 +398,38 @@
             o_work[pl.ds(pl.multiple_of(me * shard + at, 32), 32), :] = own_ref[pl.ds(at, 32), :]
 
         each(0, shard // 32, keep)
+        def settle(old):
+            for (u, qo, _, link, group), n in old:
+                def wait(s):
+                    if link == "c":
+                        ci = chip(s, u, qo, _)
+                        ref = work_rows(ci, s, 1 - c)
+                        i = ci * STREAMS + s
+                        remote(ref, ref, gcore_s.at[i], gcore_r.at[i], me).wait()
+                    else:
+                        ssem = {"p": gp_s, "q": gq_s, "u": gu_s, "d": gd_s}[link]
+                        remote(block_ref, block_ref, ssem.at[s, 2 * u + qo], gat_r.at[0], me).wait_send()
+
+                each(group * GROUP, group * GROUP + GROUP, wait)
+
+        block_ref = own_ref.at[pl.ds(0, rows)]
         rest = [t for t in sends if t[:3] != own]
+        pending = [(t, -1) for t in sends if t[:3] == own]
         seen = set()
         n = 0
         while n < len(rest):
             block, group = rest[n][:3], rest[n][4]
             links = [rest[n][3]]
+            start = n
             while n + 1 < len(rest) and rest[n + 1][:3] == block and rest[n + 1][4] == group:
                 n += 1
                 links.append(rest[n][3])
             n += 1
             new = (block, group) not in seen
             seen.add((block, group))
+            if new:
+                settle([p for p in pending if p[1] <= start - LAG])
+                pending = [p for p in pending if p[1] > start - LAG]
 
             def body(s, block=block, links=tuple(links), new=new):
                 ci = chip(s, *block)
@@ -431,10 +440,8 @@
                     send(ref, ci, s, 2 * block[0] + block[1], link)
 
             each(group * GROUP, group * GROUP + GROUP, body)
-        block_ref = own_ref.at[pl.ds(0, rows)]
-        for link, ssem in (("p", gp_s), ("q", gq_s), ("u", gu_s), ("d", gd_s)):
-            for k in sorted({2 * t[0] + t[1] for t in sends if t[3] == link}):
-                each(0, STREAMS, lambda s: remote(block_ref, block_ref, ssem.at[s, k], gat_r.at[0], me).wait_send())
+            pending += [(t, start) for t in rest[start:n]]
+        settle(pending)
 
     @pl.when(m == 0)
     def _():
@@ -443,13 +450,6 @@
     @pl.when(m == 1)
     def _():
         gather_program(MID_SENDS, (1, 0, 0))
-
-    def drain_core(i):
-        ci, s = i // STREAMS, i % STREAMS
-        ref = work_rows(ci, s, 1 - c)
-        remote(ref, ref, gcore_s.at[i], gcore_r.at[i], me).wait()
-
-    each(0, 16 * STREAMS, drain_core)
 
 
 def store_kernel(*refs):
@@ -530,7 +530,7 @@
             + [jax.ShapeDtypeStruct((total_rows, width), bf16)],
             in_specs=[vmem_spec] * 4,
             out_specs=[any_spec] * 4,
-            scratch_shapes=[dma((3 + 8,))],
+            scratch_shapes=[dma((3 + 32,))],
             compiler_params=pltpu.CompilerParams(vmem_limit_bytes=4 * 2 ** 20),
             name="store",
         )(new_master, new_first, new_second, working)

time: 401 us -> 408 us (1.017)
  Pallas kernels: 399 us -> 406 us
    pallas_call x1, Pallas kernels: 126 us -> 133 us  [device_step(): pl.pallas_call(gather_kernel, out_shape=pltpu.VMEM((total_rows, width), b...]
where the time goes in v3:
time: 408 us
  Pallas kernels  406 us (100%)
    pallas_call x1, Pallas kernels, device_step(): pl.pallas_call(reduce_kernel, out_shape=[shard, shard, shard, pltpu.VMEM(...  261 us
    pallas_call x1, Pallas kernels, device_step(): pl.pallas_call(gather_kernel, out_shape=pltpu.VMEM((total_rows, width), b...  133 us
    pallas_call x1, Pallas kernels, device_step(): pl.pallas_call(store_kernel, out_shape=[jax.ShapeDtypeStruct((shard_rows,...  13.1 us

profile of v3, /device:TPU:0, one launch (start us, length us, event | category | flops | bytes accessed | tf_op | source)
XLA Modules:
  0.0 407.7 jit_solution(1676314618053736060)
XLA Ops:
  1.3 260.7 %reduce_update.1 = (f32[1024,512]{1,0:T(8,128)S(1)}, f32[1024,512]{1,0:T(8,128)S(1)}, f32[1024,512]{1,0:T(8,128)S(1)}, bf16[1024,512]{1,0:T(8,128)(2,1)S(1)}, bf16[16384,512]{1,0:T(8,128)(2,1)}) custom-call(f32[1]{0:T(128)} %bitcast.1.lr_ref, bf16[1,32768,512]{2,1,0:T(8,128)(2,1)} %grads.1, f32[1024,512]{1,0:T(8,128)} %master.1, f32[1024,512]{1,0:T(8,128)} %mom1.1, ...), custom_call_target="tpu_custom_call" | custom-call | tf_op jit(solution)/shard_map/reduce_update/pallas_call | solution.py:481
  262.0 132.5 %gather_rows.1.refs_3_ = bf16[32768,512]{1,0:T(8,128)(2,1)S(1)} custom-call(bf16[1024,512]{1,0:T(8,128)(2,1)S(1)} %get-tuple-element.11.own_ref), custom_call_target="tpu_custom_call" | custom-call | tf_op jit(solution)/shard_map/gather_rows/pallas_call | solution.py:513
  394.5 13.1 %store.1 = (f32[1024,512]{1,0:T(8,128)}, f32[1024,512]{1,0:T(8,128)}, f32[1024,512]{1,0:T(8,128)}, bf16[32768,512]{1,0:T(8,128)(2,1)}) custom-call(f32[1024,512]{1,0:T(8,128)S(1)} %get-tuple-element.8.refs_0_, f32[1024,512]{1,0:T(8,128)S(1)} %get-tuple-element.9.refs_1_, f32[1024,512]{1,0:T(8,128)S(1)} %get-tuple-element.10.refs_2_, ...), custom_call_target="tpu_custom_call" | custom-call | tf_op jit(solution)/shard_map/store/pallas_call | solution.py:527

commit v4 on v3

--- a/solution.py
+++ b/solution.py
@@ -9,8 +9,8 @@
 MIX_RANK = 32
 DECAY_RANK = 64
 ADAM_STEP = 10
-STREAMS = 16
-GROUP = 8
+STREAMS = 8
+GROUP = 4
 LAG = 20
 MESH = pl.DeviceIdType.MESH
 
@@ -20,29 +20,29 @@
 
 
 END_JOBS = decode([
-    "f210", "f201", "u210", "f211", "f200", "f301", "u211", "f110", "u200", "f310", "u110", "u201",
-    "f300", "f311", "p310", "f011", "f100", "f111", "u300", "p311", "f101", "u111", "u301", "n011",
-    "u100", "f010", "f000", "n010", "f001", "u101", "r000", "r001",
+    "f200", "f201", "u200", "f210", "f110", "f311", "u210", "f211", "f310", "u110", "u201", "p310",
+    "p311", "f300", "f000", "u211", "f301", "f100", "u300", "f111", "f011", "u301", "u100", "n011",
+    "f010", "f101", "u111", "n010", "u101", "f001", "r000", "r001",
 ])
 MID_JOBS = decode([
-    "f211", "f311", "f310", "u311", "f010", "f011", "u310", "f300", "d011", "f200", "f210", "f101",
-    "f201", "u200", "u211", "d010", "f301", "f100", "u210", "f111", "f110", "f000", "f001", "u300",
-    "n110", "u201", "d000", "n111", "u301", "d001", "r100", "r101",
+    "f200", "f300", "f310", "f211", "f210", "f201", "u210", "f110", "f010", "u310", "f000", "u200",
+    "f311", "u311", "f011", "d010", "u300", "f111", "u211", "f001", "d011", "f301", "d000", "n110",
+    "f100", "u301", "f101", "u201", "d001", "n111", "r100", "r101",
 ])
 END_SENDS = decode([
-    "000q0", "000q1", "000u0", "000u1", "000p0", "000p1", "000c0", "000c1", "100p0", "100c1", "010u1", "010p0",
-    "200p1", "010c0", "010p1", "300p0", "300q0", "010u0", "310p0", "100p1", "201c1", "300p1", "300q1", "200p0",
-    "011c0", "001c1", "310p1", "300c1", "310c1", "100c0", "210p1", "210c1", "301c0", "301c1", "300c0", "110p1",
-    "101c1", "200c0", "200c1", "110c1", "101c0", "201c0", "001c0", "010c1", "110p0", "211c1", "110c0", "311c0",
-    "311c1", "111c1", "111c0", "310c0", "210p0", "210c0", "011c1", "211c0",
+    "000q0", "000q1", "000u0", "000u1", "000p0", "000p1", "000c0", "000c1", "010p0", "100p0", "010u0", "200p0",
+    "300p0", "100p1", "010u1", "300c0", "001c1", "010c1", "300p1", "100c0", "300q1", "011c0", "300q0", "010p1",
+    "310c0", "200p1", "100c1", "110p0", "301c0", "301c1", "201c0", "101c1", "210p0", "010c0", "310p0", "210c0",
+    "310p1", "110c0", "110p1", "310c1", "101c0", "201c1", "111c0", "200c0", "311c1", "311c0", "211c0", "200c1",
+    "110c1", "011c1", "210p1", "001c0", "300c1", "210c1", "111c1", "211c1",
 ])
 MID_SENDS = decode([
-    "100q0", "100q1", "100u0", "100u1", "100d0", "100d1", "100p0", "100p1", "100c0", "100c1", "200p0", "000p0",
-    "200d1", "000p1", "000u0", "000u1", "110u1", "101c0", "200c0", "300d0", "200d0", "200p1", "010c1", "110p1",
-    "110c1", "300p0", "300d1", "110d1", "300p1", "111c1", "201c1", "110u0", "010u0", "210d1", "110p0", "301c1",
-    "010c0", "000c1", "201c0", "001c0", "010u1", "210p1", "300c0", "210c0", "010p1", "010p0", "310c0", "110d0",
-    "111c0", "310p0", "210c1", "210p0", "300c1", "310p1", "301c0", "200c1", "101c1", "011c1", "311c0", "211c1",
-    "011c0", "210d0", "310c1", "000c0", "311c1", "211c0", "110c0", "001c1",
+    "100q0", "100q1", "100u0", "100u1", "100d0", "100d1", "100p0", "100p1", "100c0", "100c1", "000u0", "000p0",
+    "200d0", "000c1", "000p1", "200p0", "300d0", "000u1", "010p0", "110p1", "300d1", "300c1", "101c1", "110c0",
+    "110d0", "010u0", "300c0", "300p1", "200c1", "200p1", "111c1", "110u0", "110p0", "010c0", "110c1", "310p0",
+    "200d1", "001c0", "010c1", "111c0", "110u1", "101c0", "010u1", "300p0", "301c1", "310c0", "210d0", "210p0",
+    "210c0", "210p1", "110d1", "210d1", "200c0", "210c1", "001c1", "311c0", "010p1", "011c0", "211c0", "301c0",
+    "310p1", "211c1", "011c1", "000c0", "201c1", "310c1", "201c0", "311c1",
 ])
 
 
@@ -127,14 +127,12 @@
 
 
 def reduce_kernel(
-    lr_ref, grads, master, mom1, mom2,
-    o_master, o_mom1, o_mom2, o_work, praw,
+    grads, o_grad, o_clip, praw,
     stg, acc, zd, zu, fin, rb, nsum, nb, nr, nz,
-    core_s, core_r, first_s, first_r, z_s, zd_r, zu_r, q_s, pre_r, fin_r, ld, st_ld, norm_s, norm_r,
+    core_s, core_r, first_s, first_r, z_s, zd_r, zu_r, q_s, pre_r, fin_r, ld, norm_s, norm_r,
 ):
     rows, width = acc.shape[2], acc.shape[3]
     shard = STREAMS * rows
-    total_rows = grads.shape[1]
     tile = min(32, rows)
     at_dev = Place()
     me, c, m, chip, pn, qn = at_dev.me, at_dev.c, at_dev.m, at_dev.chip, at_dev.pn, at_dev.qn
@@ -209,6 +207,8 @@
             else:
                 other.wait()
             dst = stg.at[s, k] if kind == "f" else acc.at[s, k]
+            if kind == "r":
+                dst = o_grad.at[pl.ds(pl.multiple_of(s * rows, rows), rows)]
             i = s - group * GROUP
 
             def add(t):
@@ -238,17 +238,6 @@
 
         each_of(group, body)
 
-    def state_load(s):
-        at = pl.ds(pl.multiple_of(s * rows, rows), rows)
-        return [
-            pltpu.make_async_copy(src.at[at], dst.at[at], st_ld.at[i, s])
-            for i, (src, dst) in enumerate(((master, o_master), (mom1, o_mom1), (mom2, o_mom2)))
-        ]
-
-    def start_state(s):
-        for copy in state_load(s):
-            copy.start()
-
     def reduce_program(jobs, mid):
         ahead = 3
         for j in range(ahead):
@@ -260,8 +249,6 @@
             if j + 1 < len(jobs):
                 prefetch(jobs[j + 1], j + 1)
             run_job(job, j, mid)
-            if j == len(jobs) // 2:
-                each(0, STREAMS, start_state)
 
     nsum[...] = jnp.zeros_like(nsum)
 
@@ -315,20 +302,55 @@
     part = all_sum(part, z, 4, [(d, (z + i + 1) % 4) for i, d in enumerate(at_dev.zothers)], nz, nb.at[1], 8)
     square_sum = jnp.sum(part, keepdims=True)
     clip = jnp.minimum(1.0, 1.0 / (jnp.sqrt(square_sum) + 1e-6))
-    clip = jnp.broadcast_to(clip, (tile, 128))
+    o_clip[...] = jnp.broadcast_to(clip, o_clip.shape)
+    for i in range(7):
+        sent(nb.at[0], norm_s.at[i])
+    for i in range(3):
+        sent(nb.at[1], norm_s.at[8 + i])
+
+
+def gather_kernel(
+    lr_ref, grad, clip_ref, master, mom1, mom2, o_master, o_mom1, o_mom2, o_work, st_ld, gat_r, gcore_r, gcore_s, gp_s, gu_s, gd_s, gq_s,
+):
+    shard, width = grad.shape
+    total_rows = o_work.shape[0]
+    rows = shard // STREAMS
+    tile = min(32, rows)
+    at_dev = Place()
+    me, c, m, chip = at_dev.me, at_dev.c, at_dev.m, at_dev.chip
+    my_chip = me // 2
+
+    others = [at_dev.partner, at_dev.xn, at_dev.yn] + at_dev.zothers
+    barrier = pltpu.get_barrier_semaphore()
+    for other in others:
+        pl.semaphore_signal(barrier, inc=1, device_id=(other,), device_id_type=MESH)
+
+    def state_load(s):
+        at = pl.ds(pl.multiple_of(s * rows, rows), rows)
+        return [
+            pltpu.make_async_copy(src.at[at], dst.at[at], st_ld.at[i, s])
+            for i, (src, dst) in enumerate(((master, o_master), (mom1, o_mom1), (mom2, o_mom2)))
+        ]
+
+    def start_state(s):
+        for copy in state_load(s):
+            copy.start()
+
+    each(0, STREAMS, start_state)
 
     learn_rate = lr_ref[0]
     inv1 = 1.0 / (1.0 - 0.9 ** ADAM_STEP)
     inv2 = 1.0 / (1.0 - 0.99 ** ADAM_STEP)
     decay_runs, fast_rows = rule_runs(width, total_rows)
 
+    clip = jnp.broadcast_to(clip_ref[0:1, :], (tile, 128))
+
     def update(s):
         for copy in state_load(s):
             copy.wait()
 
         def rows_step(t):
             base = pl.multiple_of(t * tile, tile)
-            at = pl.ds(base, tile)
             out_at = pl.ds(pl.multiple_of(s * rows + t * tile, tile), tile)
             row = me * shard + s * rows + base + lax.broadcasted_iota(jnp.int32, (tile, 128), 0)
             decays = (row >= decay_runs[0][0]) & (row < decay_runs[0][1])
@@ -341,7 +363,7 @@
             step_size = learn_rate * jnp.where(fast, 2.0, 1.0)
             for col in range(0, width, 128):
                 cols = pl.ds(col, 128)
-                g = acc[s, 2 * m, at, cols] * clip
+                g = grad[out_at, cols] * clip
                 old = o_master[out_at, cols]
                 first = 0.9 * o_mom1[out_at, cols] + 0.1 * g
                 second = 0.99 * o_mom2[out_at, cols] + 0.01 * (g * g)
@@ -349,26 +371,12 @@
                 o_master[out_at, cols] = new
                 o_mom1[out_at, cols] = first
                 o_mom2[out_at, cols] = second
-                o_work[out_at, cols] = new.astype(jnp.bfloat16)
+                o_work[pl.ds(pl.multiple_of(me * shard + s * rows + base, tile), tile), cols] = new.astype(jnp.bfloat16)
 
         each(0, rows // tile, rows_step)
 
-    each(0, STREAMS, update)
-
-    for i in range(7):
-        sent(nb.at[0], norm_s.at[i])
-    for i in range(3):
-        sent(nb.at[1], norm_s.at[8 + i])
-
-
-def gather_kernel(own_ref, o_work, own_s, gat_r, gcore_r, gcore_s, gp_s, gu_s, gd_s, gq_s):
-    shard, width = own_ref.shape
-    rows = shard // STREAMS
-    at_dev = Place()
-    me, c, m, chip = at_dev.me, at_dev.c, at_dev.m, at_dev.chip
-    my_chip = me // 2
-
-    enter([at_dev.partner, at_dev.xn, at_dev.yn] + at_dev.zothers)
+    update(0)
+    pl.semaphore_wait(barrier, len(others))
 
     def work_rows(ci, s, cc):
         return o_work.at[pl.ds(pl.multiple_of((ci * 2 + cc) * shard + s * rows, rows), rows)]
@@ -387,17 +395,18 @@
         first = [t for t in sends if t[:3] == own and t[4] == 0]
 
         def start_own(s):
-            src = own_ref.at[pl.ds(pl.multiple_of(s * rows, rows), rows)]
+            src = work_rows(my_chip, s, c)
             for u, qo, _, link, _ in first:
                 send(src, my_chip, s, 2 * u + qo, link)
 
-        each(0, STREAMS, start_own)
-
-        def keep(t):
-            at = pl.multiple_of(t * 32, 32)
-            o_work[pl.ds(pl.multiple_of(me * shard + at, 32), 32), :] = own_ref[pl.ds(at, 32), :]
-
-        each(0, shard // 32, keep)
+        start_own(0)
+
+        def rest_own(s):
+            update(s)
+            start_own(s)
+
+        each(1, STREAMS, rest_own)
+
         def settle(old):
             for (u, qo, _, link, group), n in old:
                 def wait(s):
@@ -412,7 +421,7 @@
 
                 each(group * GROUP, group * GROUP + GROUP, wait)
 
-        block_ref = own_ref.at[pl.ds(0, rows)]
+        block_ref = o_work.at[pl.ds(0, rows)]
         rest = [t for t in sends if t[:3] != own]
         pending = [(t, -1) for t in sends if t[:3] == own]
         seen = set()
@@ -475,18 +484,19 @@
         rows = shard_rows // STREAMS
         any_spec = pl.BlockSpec(memory_space=pl.ANY)
         vmem_spec = pl.BlockSpec(memory_space=pltpu.VMEM)
+        hbm_spec = pl.BlockSpec(memory_space=pltpu.HBM)
         dma = pltpu.SemaphoreType.DMA
         f32, bf16 = jnp.float32, jnp.bfloat16
         shard = pltpu.VMEM((shard_rows, width), f32)
-        new_master, new_first, new_second, own_rows, _ = pl.pallas_call(
+        grad_rows, clip, _ = pl.pallas_call(
             reduce_kernel,
             out_shape=[
-                shard, shard, shard,
-                pltpu.VMEM((shard_rows, width), bf16),
+                shard,
+                pltpu.VMEM((8, 128), f32),
                 jax.ShapeDtypeStruct((total_rows // 2, width), bf16),
             ],
-            in_specs=[pl.BlockSpec(memory_space=pltpu.SMEM)] + [any_spec] * 4,
-            out_specs=[vmem_spec] * 4 + [any_spec],
+            in_specs=[any_spec],
+            out_specs=[vmem_spec] * 2 + [any_spec],
             scratch_shapes=[
                 pltpu.VMEM((STREAMS, 8, rows, width), f32),
                 pltpu.VMEM((STREAMS, 8, rows, width), f32),
@@ -502,28 +512,28 @@
                 dma((STREAMS, 8)), dma((STREAMS, 8)),
                 dma((STREAMS, 8)), dma((STREAMS, 5)), dma((STREAMS, 4)),
                 dma((STREAMS, 2)), dma((STREAMS,)), dma((STREAMS,)),
-                dma((2, GROUP, 2)), dma((3, STREAMS)),
+                dma((2, GROUP, 2)),
                 dma((12,)), dma((12,)),
             ],
             compiler_params=pltpu.CompilerParams(
                 collective_id=0, has_side_effects=True, vmem_limit_bytes=56 * 2 ** 20
             ),
-            name="reduce_update",
-        )(learn_rate.reshape(1), local_grads, master, mom_first, mom_second)
-        working = pl.pallas_call(
+            name="reduce_rows",
+        )(local_grads)
+        new_master, new_first, new_second, working = pl.pallas_call(
             gather_kernel,
-            out_shape=pltpu.VMEM((total_rows, width), bf16),
-            in_specs=[vmem_spec],
-            out_specs=vmem_spec,
+            out_shape=[shard, shard, shard, pltpu.VMEM((total_rows, width), bf16)],
+            in_specs=[pl.BlockSpec(memory_space=pltpu.SMEM)] + [vmem_spec] * 2 + [hbm_spec] * 3,
+            out_specs=[vmem_spec] * 4,
             scratch_shapes=[
-                dma((STREAMS,)), dma((16 * STREAMS,)), dma((16 * STREAMS,)), dma((16 * STREAMS,)),
+                dma((3, STREAMS)), dma((16 * STREAMS,)), dma((16 * STREAMS,)), dma((16 * STREAMS,)),
                 dma((STREAMS, 8)), dma((STREAMS, 8)), dma((STREAMS, 8)), dma((STREAMS, 8)),
             ],
             compiler_params=pltpu.CompilerParams(
                 collective_id=1, has_side_effects=True, vmem_limit_bytes=4 * 2 ** 20
             ),
-            name="gather_rows",
-        )(own_rows)
+            name="update_gather",
+        )(learn_rate.reshape(1), grad_rows, clip, master, mom_first, mom_second)
         return pl.pallas_call(
             store_kernel,
             out_shape=[jax.ShapeDtypeStruct((shard_rows, width), f32)] * 3

time: 408 us -> 395 us (0.968)
  Pallas kernels: 406 us -> 392 us
    pallas_call x2, Pallas kernels: 393 us -> 379 us  [the longest x1 252 us: device_step(): pl.pallas_call(reduce_kernel, out_shape=[shard, pltpu.VMEM((8, 128), f32)...]
where the time goes in v4:
time: 395 us
  Pallas kernels  392 us (99%)
    pallas_call x1, Pallas kernels, device_step(): pl.pallas_call(reduce_kernel, out_shape=[shard, pltpu.VMEM((8, 128), f32)...  252 us
    pallas_call x1, Pallas kernels, device_step(): pl.pallas_call(gather_kernel, out_shape=[shard, shard, shard, pltpu.VMEM(...  126 us
    pallas_call x1, Pallas kernels, device_step(): pl.pallas_call(store_kernel, out_shape=[jax.ShapeDtypeStruct((shard_rows,...  13.1 us

profile of v4, /device:TPU:0, one launch (start us, length us, event | category | flops | bytes accessed | tf_op | source)
XLA Modules:
  0.0 394.7 jit_solution(1592359355594654088)
XLA Ops:
  1.3 0.0 copy-start
  1.3 0.0 copy-start.1
  1.3 252.4 %reduce_rows.1 = (f32[1024,512]{1,0:T(8,128)S(1)}, f32[8,128]{1,0:T(8,128)S(1)}, bf16[16384,512]{1,0:T(8,128)(2,1)}) custom-call(bf16[1,32768,512]{2,1,0:T(8,128)(2,1)} %grads.1), custom_call_target="tpu_custom_call" | custom-call | tf_op jit(solution)/shard_map/reduce_rows/pallas_call | solution.py:491
  253.8 0.0 copy-done
  253.8 0.0 copy-done.1
  253.8 0.0 copy-start.2
  253.8 1.6 copy-done.2
  255.4 126.3 %update_gather.1 = (f32[1024,512]{1,0:T(8,128)S(1)}, f32[1024,512]{1,0:T(8,128)S(1)}, f32[1024,512]{1,0:T(8,128)S(1)}, bf16[32768,512]{1,0:T(8,128)(2,1)S(1)}) custom-call(f32[1]{0:T(128)} %bitcast.1.lr_ref, f32[1024,512]{1,0:T(8,128)S(1)} %get-tuple-element.10.grad, f32[8,128]{1,0:T(8,128)S(1)} %get-tuple-element.11.clip_ref, f32[1024,512]{1,0:T(8,128)S(1)} %copy-done, ...), custom_call_target="tpu_custom_call" | custom-call | tf_op jit(solution)/shard_map/update_gather/pallas_call | solution.py:523
  381.6 13.1 %store.1 = (f32[1024,512]{1,0:T(8,128)}, f32[1024,512]{1,0:T(8,128)}, f32[1024,512]{1,0:T(8,128)}, bf16[32768,512]{1,0:T(8,128)(2,1)}) custom-call(f32[1024,512]{1,0:T(8,128)S(1)} %get-tuple-element.12.refs_0_, f32[1024,512]{1,0:T(8,128)S(1)} %get-tuple-element.13.refs_1_, f32[1024,512]{1,0:T(8,128)S(1)} %get-tuple-element.14.refs_2_, ...), custom_call_target="tpu_custom_call" | custom-call | tf_op jit(solution)/shard_map/store/pallas_call | solution.py:537
Async XLA Ops:
  1.3 252.5 %copy-start = (f32[1024,512]{1,0:T(8,128)S(1)}, f32[1024,512]{1,0:T(8,128)}, u32[]{:S(2)}) copy-start(f32[1024,512]{1,0:T(8,128)} %master.1) | copy-start | bytes 6291460
  1.3 252.5 %copy-start.1 = (f32[1024,512]{1,0:T(8,128)S(1)}, f32[1024,512]{1,0:T(8,128)}, u32[]{:S(2)}) copy-start(f32[1024,512]{1,0:T(8,128)} %mom1.1) | copy-start | bytes 6291460
  253.8 1.6 copy-start.2

commit v5 on v4

--- a/solution.py
+++ b/solution.py
@@ -101,19 +101,29 @@
         return ((zz * 2 + yy) * 2 + xx) * 2 + cc
 
     def pn(self, s):
+        if isinstance(s, int):
+            return self.yn if s % 2 else self.xn
         h = s % 2
         return self.xn * (1 - h) + self.yn * h
 
     def qn(self, s):
+        if isinstance(s, int):
+            return self.xn if s % 2 else self.yn
         h = s % 2
         return self.yn * (1 - h) + self.xn * h
 
     def chip(self, s, u, qo, po):
         h = s % 2
-        first = self.x * (1 - h) + self.y * h
-        last = self.y * (1 - h) + self.x * h
+        if isinstance(s, int):
+            first, last = (self.y, self.x) if h else (self.x, self.y)
+        else:
+            first = self.x * (1 - h) + self.y * h
+            last = self.y * (1 - h) + self.x * h
         pv = 1 - first if po else first
         qv = 1 - last if qo else last
+        if isinstance(s, int):
+            xx, yy = (qv, pv) if s % 2 else (pv, qv)
+            return ((self.lo * u + (1 - self.lo) * (3 - u)) * 2 + yy) * 2 + xx
         xx = pv * (1 - h) + qv * h
         yy = qv * (1 - h) + pv * h
         return ((self.lo * u + (1 - self.lo) * (3 - u)) * 2 + yy) * 2 + xx
@@ -310,7 +320,7 @@
 
 
 def gather_kernel(
-    lr_ref, grad, clip_ref, master, mom1, mom2, o_master, o_mom1, o_mom2, o_work, st_ld, gat_r, gcore_r, gcore_s, gp_s, gu_s, gd_s, gq_s,
+    lr_ref, grad, clip_ref, master, mom1, mom2, o_master, o_mom1, o_mom2, o_work, gat_r, gcore_r, gcore_s, gp_s, gu_s, gd_s, gq_s,
 ):
     shard, width = grad.shape
     total_rows = o_work.shape[0]
@@ -325,19 +335,6 @@
     for other in others:
         pl.semaphore_signal(barrier, inc=1, device_id=(other,), device_id_type=MESH)
 
-    def state_load(s):
-        at = pl.ds(pl.multiple_of(s * rows, rows), rows)
-        return [
-            pltpu.make_async_copy(src.at[at], dst.at[at], st_ld.at[i, s])
-            for i, (src, dst) in enumerate(((master, o_master), (mom1, o_mom1), (mom2, o_mom2)))
-        ]
-
-    def start_state(s):
-        for copy in state_load(s):
-            copy.start()
-
-    each(0, STREAMS, start_state)
-
     learn_rate = lr_ref[0]
     inv1 = 1.0 / (1.0 - 0.9 ** ADAM_STEP)
     inv2 = 1.0 / (1.0 - 0.99 ** ADAM_STEP)
@@ -346,9 +343,6 @@
     clip = jnp.broadcast_to(clip_ref[0:1, :], (tile, 128))
 
     def update(s):
-        for copy in state_load(s):
-            copy.wait()
-
         def rows_step(t):
             base = pl.multiple_of(t * tile, tile)
             out_at = pl.ds(pl.multiple_of(s * rows + t * tile, tile), tile)
@@ -364,9 +358,9 @@
             for col in range(0, width, 128):
                 cols = pl.ds(col, 128)
                 g = grad[out_at, cols] * clip
-                old = o_master[out_at, cols]
-                first = 0.9 * o_mom1[out_at, cols] + 0.1 * g
-                second = 0.99 * o_mom2[out_at, cols] + 0.01 * (g * g)
+                old = master[out_at, cols]
+                first = 0.9 * mom1[out_at, cols] + 0.1 * g
+                second = 0.99 * mom2[out_at, cols] + 0.01 * (g * g)
                 new = old - step_size * ((first * inv1) / (jnp.sqrt(second * inv2) + 1e-8) + decay * old)
                 o_master[out_at, cols] = new
                 o_mom1[out_at, cols] = first
@@ -448,7 +442,8 @@
                 for link in links:
                     send(ref, ci, s, 2 * block[0] + block[1], link)
 
-            each(group * GROUP, group * GROUP + GROUP, body)
+            for s in range(group * GROUP, group * GROUP + GROUP):
+                body(s)
             pending += [(t, start) for t in rest[start:n]]
         settle(pending)
 
@@ -484,7 +479,6 @@
         rows = shard_rows // STREAMS
         any_spec = pl.BlockSpec(memory_space=pl.ANY)
         vmem_spec = pl.BlockSpec(memory_space=pltpu.VMEM)
-        hbm_spec = pl.BlockSpec(memory_space=pltpu.HBM)
         dma = pltpu.SemaphoreType.DMA
         f32, bf16 = jnp.float32, jnp.bfloat16
         shard = pltpu.VMEM((shard_rows, width), f32)
@@ -516,17 +510,17 @@
                 dma((12,)), dma((12,)),
             ],
             compiler_params=pltpu.CompilerParams(
-                collective_id=0, has_side_effects=True, vmem_limit_bytes=56 * 2 ** 20
+                collective_id=0, has_side_effects=True, vmem_limit_bytes=217 * 2 ** 18
             ),
             name="reduce_rows",
         )(local_grads)
         new_master, new_first, new_second, working = pl.pallas_call(
             gather_kernel,
             out_shape=[shard, shard, shard, pltpu.VMEM((total_rows, width), bf16)],
-            in_specs=[pl.BlockSpec(memory_space=pltpu.SMEM)] + [vmem_spec] * 2 + [hbm_spec] * 3,
+            in_specs=[pl.BlockSpec(memory_space=pltpu.SMEM)] + [vmem_spec] * 5,
             out_specs=[vmem_spec] * 4,
             scratch_shapes=[
-                dma((3, STREAMS)), dma((16 * STREAMS,)), dma((16 * STREAMS,)), dma((16 * STREAMS,)),
+                dma((16 * STREAMS,)), dma((16 * STREAMS,)), dma((16 * STREAMS,)),
                 dma((STREAMS, 8)), dma((STREAMS, 8)), dma((STREAMS, 8)), dma((STREAMS, 8)),
             ],
             compiler_params=pltpu.CompilerParams(

time: 395 us -> 393 us (level)
  no operation moved by 1% of the time
where the time goes in v5:
time: 393 us
  Pallas kernels  392 us (100%)
    pallas_call x1, Pallas kernels, device_step(): pl.pallas_call(reduce_kernel, out_shape=[shard, pltpu.VMEM((8, 128), f32)...  252 us
    pallas_call x1, Pallas kernels, device_step(): pl.pallas_call(gather_kernel, out_shape=[shard, shard, shard, pltpu.VMEM(...  126 us
    pallas_call x1, Pallas kernels, device_step(): pl.pallas_call(store_kernel, out_shape=[jax.ShapeDtypeStruct((shard_rows,...  13.1 us

profile of v5, /device:TPU:0, one launch (start us, length us, event | category | flops | bytes accessed | tf_op | source)
XLA Modules:
  0.0 393.0 jit_solution(142417445744466817)
XLA Ops:
  1.3 0.0 copy-start
  1.3 0.0 copy-start.1
  1.3 0.0 copy-start.2
  1.3 252.4 %reduce_rows.1 = (f32[1024,512]{1,0:T(8,128)S(1)}, f32[8,128]{1,0:T(8,128)S(1)}, bf16[16384,512]{1,0:T(8,128)(2,1)}) custom-call(bf16[1,32768,512]{2,1,0:T(8,128)(2,1)} %grads.1), custom_call_target="tpu_custom_call" | custom-call | tf_op jit(solution)/shard_map/reduce_rows/pallas_call | solution.py:485
  253.8 0.0 copy-done
  253.8 0.0 copy-done.1
  253.8 0.0 copy-done.2
  253.8 126.1 %update_gather.1 = (f32[1024,512]{1,0:T(8,128)S(1)}, f32[1024,512]{1,0:T(8,128)S(1)}, f32[1024,512]{1,0:T(8,128)S(1)}, bf16[32768,512]{1,0:T(8,128)(2,1)S(1)}) custom-call(f32[1]{0:T(128)} %bitcast.1.lr_ref, f32[1024,512]{1,0:T(8,128)S(1)} %get-tuple-element.10.grad, f32[8,128]{1,0:T(8,128)S(1)} %get-tuple-element.11.clip_ref, f32[1024,512]{1,0:T(8,128)S(1)} %copy-done, ...), custom_call_target="tpu_custom_call" | custom-call | tf_op jit(solution)/shard_map/update_gather/pallas_call | solution.py:517
  379.9 13.1 %store.1 = (f32[1024,512]{1,0:T(8,128)}, f32[1024,512]{1,0:T(8,128)}, f32[1024,512]{1,0:T(8,128)}, bf16[32768,512]{1,0:T(8,128)(2,1)}) custom-call(f32[1024,512]{1,0:T(8,128)S(1)} %get-tuple-element.12.refs_0_, f32[1024,512]{1,0:T(8,128)S(1)} %get-tuple-element.13.refs_1_, f32[1024,512]{1,0:T(8,128)S(1)} %get-tuple-element.14.refs_2_, ...), custom_call_target="tpu_custom_call" | custom-call | tf_op jit(solution)/shard_map/store/pallas_call | solution.py:531
Async XLA Ops:
  1.3 252.5 %copy-start = (f32[1024,512]{1,0:T(8,128)S(1)}, f32[1024,512]{1,0:T(8,128)}, u32[]{:S(2)}) copy-start(f32[1024,512]{1,0:T(8,128)} %master.1) | copy-start | bytes 6291460
  1.3 252.5 %copy-start.1 = (f32[1024,512]{1,0:T(8,128)S(1)}, f32[1024,512]{1,0:T(8,128)}, u32[]{:S(2)}) copy-start(f32[1024,512]{1,0:T(8,128)} %mom1.1) | copy-start | bytes 6291460
  1.3 252.5 %copy-start.2 = (f32[1024,512]{1,0:T(8,128)S(1)}, f32[1024,512]{1,0:T(8,128)}, u32[]{:S(2)}) copy-start(f32[1024,512]{1,0:T(8,128)} %mom2.1) | copy-start | bytes 6291460

commit v6 on v5

--- a/solution.py
+++ b/solution.py
@@ -20,14 +20,14 @@
 
 
 END_JOBS = decode([
-    "f200", "f201", "u200", "f210", "f110", "f311", "u210", "f211", "f310", "u110", "u201", "p310",
-    "p311", "f300", "f000", "u211", "f301", "f100", "u300", "f111", "f011", "u301", "u100", "n011",
-    "f010", "f101", "u111", "n010", "u101", "f001", "r000", "r001",
+    "f200", "f211", "u200", "f201", "u211", "f210", "f110", "u210", "f310", "f300", "u110", "f311",
+    "f100", "p310", "u201", "f301", "u300", "f111", "p311", "u111", "f000", "u301", "f011", "f101",
+    "u100", "f010", "n010", "n011", "f001", "u101", "r000", "r001",
 ])
 MID_JOBS = decode([
-    "f200", "f300", "f310", "f211", "f210", "f201", "u210", "f110", "f010", "u310", "f000", "u200",
-    "f311", "u311", "f011", "d010", "u300", "f111", "u211", "f001", "d011", "f301", "d000", "n110",
-    "f100", "u301", "f101", "u201", "d001", "n111", "r100", "r101",
+    "f301", "f211", "f311", "f110", "f210", "f310", "f300", "f011", "u211", "f201", "u310", "f010",
+    "u311", "u210", "f200", "f001", "d010", "f000", "f101", "u300", "u200", "d000", "f100", "f111",
+    "d011", "n110", "u301", "d001", "u201", "n111", "r100", "r101",
 ])
 END_SENDS = decode([
     "000q0", "000q1", "000u0", "000u1", "000p0", "000p1", "000c0", "000c1", "010p0", "100p0", "010u0", "200p0",
@@ -139,11 +139,11 @@
 def reduce_kernel(
     grads, o_grad, o_clip, praw,
     stg, acc, zd, zu, fin, rb, nsum, nb, nr, nz,
-    core_s, core_r, first_s, first_r, z_s, zd_r, zu_r, q_s, pre_r, fin_r, ld, norm_s, norm_r,
+    core_s, core_r, first_s, first_r, half_r, z_s, zd_r, zu_r, q_s, pre_r, fin_r, ld, norm_s, norm_r,
 ):
     rows, width = acc.shape[2], acc.shape[3]
     shard = STREAMS * rows
-    tile = min(32, rows)
+    tile = min(32, rows // 2)
     at_dev = Place()
     me, c, m, chip, pn, qn = at_dev.me, at_dev.c, at_dev.m, at_dev.chip, at_dev.pn, at_dev.qn
 
@@ -195,6 +195,9 @@
         kind, u, qo, group = job
         k = 2 * u + qo
         slot = j % 2
+        early = not mid and job[1:] == END_JOBS[0][1:]
+        pieces = 2 if early and kind in ("f", "u") else 1
+        size = rows // pieces
 
         def body(s):
             own, core, other = loads(job, j, s)
@@ -209,13 +212,6 @@
                     parts.append((zd.at[s, 0], pre_r.at[s]))
                 if kind == "r":
                     parts.append((fin.at[s], fin_r.at[s]))
-            for ref, rsem in parts:
-                landed(ref, rsem)
-            own.wait()
-            if other is None:
-                core.wait_recv()
-            else:
-                other.wait()
             dst = stg.at[s, k] if kind == "f" else acc.at[s, k]
             if kind == "r":
                 dst = o_grad.at[pl.ds(pl.multiple_of(s * rows, rows), rows)]
@@ -231,20 +227,35 @@
                     nsum[...] += jnp.sum((v * v).reshape(tile // 8, 8, width), axis=0)
                 dst[at, :] = v
 
-            each(0, rows // tile, add)
-            if kind == "f":
-                remote(dst, acc.at[s, k], first_s.at[s, k], first_r.at[s, k], pn(s)).start()
-            elif kind == "p":
-                remote(dst, zd.at[s, 0], q_s.at[s, 0], pre_r.at[s], qn(s)).start()
-            elif kind == "n":
-                remote(dst, fin.at[s], q_s.at[s, 1], fin_r.at[s], qn(s)).start()
-            elif kind == "u" and not mid:
-                remote(dst, zd.at[s, k - 2], z_s.at[s, k], zd_r.at[s, k - 2], at_dev.up).start()
-            elif kind == "u":
-                kk = 2 * (3 - u) + qo
-                remote(dst, zu.at[s, kk], z_s.at[s, k], zu_r.at[s, kk], at_dev.up).start()
-            elif kind == "d":
-                remote(dst, zu.at[s, k], z_s.at[s, k], zu_r.at[s, k], at_dev.down).start()
+            for piece in range(pieces):
+                cut = pl.ds(piece * size, size)
+                for n, (ref, rsem) in enumerate(parts):
+                    if n == 0 and early:
+                        landed(ref.at[cut], half_r.at[s] if piece else rsem)
+                    elif piece == 0:
+                        landed(ref, rsem)
+                if piece == 0:
+                    own.wait()
+                    if other is None:
+                        core.wait_recv()
+                    else:
+                        other.wait()
+                each(piece * size // tile, (piece + 1) * size // tile, add)
+                src = dst.at[cut]
+                if kind == "f":
+                    rsem = half_r.at[s] if piece else first_r.at[s, k]
+                    remote(src, acc.at[s, k].at[cut], first_s.at[s, k], rsem, pn(s)).start()
+                elif kind == "p":
+                    remote(src, zd.at[s, 0], q_s.at[s, 0], pre_r.at[s], qn(s)).start()
+                elif kind == "n":
+                    remote(src, fin.at[s], q_s.at[s, 1], fin_r.at[s], qn(s)).start()
+                elif kind == "u" and not mid:
+                    remote(src, zd.at[s, k - 2].at[cut], z_s.at[s, k], zd_r.at[s, k - 2], at_dev.up).start()
+                elif kind == "u":
+                    kk = 2 * (3 - u) + qo
+                    remote(src, zu.at[s, kk], z_s.at[s, k], zu_r.at[s, kk], at_dev.up).start()
+                elif kind == "d":
+                    remote(src, zu.at[s, k], z_s.at[s, k], zu_r.at[s, k], at_dev.down).start()
 
         each_of(group, body)
 
@@ -503,7 +514,7 @@
                 pltpu.VMEM((8, 8, 128), f32),
                 pltpu.VMEM((4, 8, 128), f32),
                 dma((16 * STREAMS,)), dma((16 * STREAMS,)),
-                dma((STREAMS, 8)), dma((STREAMS, 8)),
+                dma((STREAMS, 8)), dma((STREAMS, 8)), dma((STREAMS,)),
                 dma((STREAMS, 8)), dma((STREAMS, 5)), dma((STREAMS, 4)),
                 dma((STREAMS, 2)), dma((STREAMS,)), dma((STREAMS,)),
                 dma((2, GROUP, 2)),
@@ -534,7 +545,7 @@
             + [jax.ShapeDtypeStruct((total_rows, width), bf16)],
             in_specs=[vmem_spec] * 4,
             out_specs=[any_spec] * 4,
-            scratch_shapes=[dma((3 + 32,))],
+            scratch_shapes=[dma((3 + 8,))],
             compiler_params=pltpu.CompilerParams(vmem_limit_bytes=4 * 2 ** 20),
             name="store",
         )(new_master, new_first, new_second, working)

time: 393 us -> 390 us (level)
  no operation moved by 1% of the time
where the time goes in v6:
time: 390 us
  Pallas kernels  389 us (100%)
    pallas_call x1, Pallas kernels, device_step(): pl.pallas_call(reduce_kernel, out_shape=[shard, pltpu.VMEM((8, 128), f32)...  250 us
    pallas_call x1, Pallas kernels, device_step(): pl.pallas_call(gather_kernel, out_shape=[shard, shard, shard, pltpu.VMEM(...  126 us
    pallas_call x1, Pallas kernels, device_step(): pl.pallas_call(store_kernel, out_shape=[jax.ShapeDtypeStruct((shard_rows,...  13 us

profile of v6, /device:TPU:0, one launch (start us, length us, event | category | flops | bytes accessed | tf_op | source)
XLA Modules:
  0.0 390.1 jit_solution(224569540558555884)
XLA Ops:
  1.3 0.0 copy-start
  1.3 0.0 copy-start.1
  1.3 0.0 copy-start.2
  1.3 249.6 %reduce_rows.1 = (f32[1024,512]{1,0:T(8,128)S(1)}, f32[8,128]{1,0:T(8,128)S(1)}, bf16[16384,512]{1,0:T(8,128)(2,1)}) custom-call(bf16[1,32768,512]{2,1,0:T(8,128)(2,1)} %grads.1), custom_call_target="tpu_custom_call" | custom-call | tf_op jit(solution)/shard_map/reduce_rows/pallas_call | solution.py:496
  250.9 0.0 copy-done
  251.0 0.0 copy-done.1
  251.0 0.0 copy-done.2
  251.0 126.2 %update_gather.1 = (f32[1024,512]{1,0:T(8,128)S(1)}, f32[1024,512]{1,0:T(8,128)S(1)}, f32[1024,512]{1,0:T(8,128)S(1)}, bf16[32768,512]{1,0:T(8,128)(2,1)S(1)}) custom-call(f32[1]{0:T(128)} %bitcast.1.lr_ref, f32[1024,512]{1,0:T(8,128)S(1)} %get-tuple-element.10.grad, f32[8,128]{1,0:T(8,128)S(1)} %get-tuple-element.11.clip_ref, f32[1024,512]{1,0:T(8,128)S(1)} %copy-done, ...), custom_call_target="tpu_custom_call" | custom-call | tf_op jit(solution)/shard_map/update_gather/pallas_call | solution.py:528
  377.1 13.0 %store.1 = (f32[1024,512]{1,0:T(8,128)}, f32[1024,512]{1,0:T(8,128)}, f32[1024,512]{1,0:T(8,128)}, bf16[32768,512]{1,0:T(8,128)(2,1)}) custom-call(f32[1024,512]{1,0:T(8,128)S(1)} %get-tuple-element.12.refs_0_, f32[1024,512]{1,0:T(8,128)S(1)} %get-tuple-element.13.refs_1_, f32[1024,512]{1,0:T(8,128)S(1)} %get-tuple-element.14.refs_2_, ...), custom_call_target="tpu_custom_call" | custom-call | tf_op jit(solution)/shard_map/store/pallas_call | solution.py:542
Async XLA Ops:
  1.3 249.7 %copy-start = (f32[1024,512]{1,0:T(8,128)S(1)}, f32[1024,512]{1,0:T(8,128)}, u32[]{:S(2)}) copy-start(f32[1024,512]{1,0:T(8,128)} %master.1) | copy-start | bytes 6291460
  1.3 249.7 %copy-start.1 = (f32[1024,512]{1,0:T(8,128)S(1)}, f32[1024,512]{1,0:T(8,128)}, u32[]{:S(2)}) copy-start(f32[1024,512]{1,0:T(8,128)} %mom1.1) | copy-start | bytes 6291460
  1.3 249.7 %copy-start.2 = (f32[1024,512]{1,0:T(8,128)S(1)}, f32[1024,512]{1,0:T(8,128)}, u32[]{:S(2)}) copy-start(f32[1024,512]{1,0:T(8,128)} %mom2.1) | copy-start | bytes 6291460

commit v7 on v6

--- a/solution.py
+++ b/solution.py
@@ -341,10 +341,13 @@
     me, c, m, chip = at_dev.me, at_dev.c, at_dev.m, at_dev.chip
     my_chip = me // 2
 
-    others = [at_dev.partner, at_dev.xn, at_dev.yn] + at_dev.zothers
     barrier = pltpu.get_barrier_semaphore()
-    for other in others:
+    for other in (at_dev.partner, at_dev.xn, at_dev.yn, at_dev.up):
         pl.semaphore_signal(barrier, inc=1, device_id=(other,), device_id_type=MESH)
+
+    @pl.when(m == 1)
+    def _():
+        pl.semaphore_signal(barrier, inc=1, device_id=(at_dev.down,), device_id_type=MESH)
 
     learn_rate = lr_ref[0]
     inv1 = 1.0 / (1.0 - 0.9 ** ADAM_STEP)
@@ -381,7 +384,7 @@
         each(0, rows // tile, rows_step)
 
     update(0)
-    pl.semaphore_wait(barrier, len(others))
+    pl.semaphore_wait(barrier, 4 + m)
 
     def work_rows(ci, s, cc):
         return o_work.at[pl.ds(pl.multiple_of((ci * 2 + cc) * shard + s * rows, rows), rows)]

time: 390 us -> 390 us (level)
  no operation moved by 1% of the time
where the time goes in v7:
time: 390 us
  Pallas kernels  388 us (99%)
    pallas_call x1, Pallas kernels, device_step(): pl.pallas_call(reduce_kernel, out_shape=[shard, pltpu.VMEM((8, 128), f32)...  250 us
    pallas_call x1, Pallas kernels, device_step(): pl.pallas_call(gather_kernel, out_shape=[shard, shard, shard, pltpu.VMEM(...  126 us
    pallas_call x1, Pallas kernels, device_step(): pl.pallas_call(store_kernel, out_shape=[jax.ShapeDtypeStruct((shard_rows,...  13 us

profile of v7, /device:TPU:0, one launch (start us, length us, event | category | flops | bytes accessed | tf_op | source)
XLA Modules:
  0.0 389.7 jit_solution(2778224604093671911)
XLA Ops:
  1.3 0.0 copy-start
  1.3 0.0 copy-start.1
  1.3 0.0 copy-start.2
  1.3 249.6 %reduce_rows.1 = (f32[1024,512]{1,0:T(8,128)S(1)}, f32[8,128]{1,0:T(8,128)S(1)}, bf16[16384,512]{1,0:T(8,128)(2,1)}) custom-call(bf16[1,32768,512]{2,1,0:T(8,128)(2,1)} %grads.1), custom_call_target="tpu_custom_call" | custom-call | tf_op jit(solution)/shard_map/reduce_rows/pallas_call | solution.py:499
  250.9 0.0 copy-done
  251.0 0.0 copy-done.1
  251.0 0.0 copy-done.2
  251.0 125.7 %update_gather.1 = (f32[1024,512]{1,0:T(8,128)S(1)}, f32[1024,512]{1,0:T(8,128)S(1)}, f32[1024,512]{1,0:T(8,128)S(1)}, bf16[32768,512]{1,0:T(8,128)(2,1)S(1)}) custom-call(f32[1]{0:T(128)} %bitcast.1.lr_ref, f32[1024,512]{1,0:T(8,128)S(1)} %get-tuple-element.10.grad, f32[8,128]{1,0:T(8,128)S(1)} %get-tuple-element.11.clip_ref, f32[1024,512]{1,0:T(8,128)S(1)} %copy-done, ...), custom_call_target="tpu_custom_call" | custom-call | tf_op jit(solution)/shard_map/update_gather/pallas_call | solution.py:531
  376.7 13.0 %store.1 = (f32[1024,512]{1,0:T(8,128)}, f32[1024,512]{1,0:T(8,128)}, f32[1024,512]{1,0:T(8,128)}, bf16[32768,512]{1,0:T(8,128)(2,1)}) custom-call(f32[1024,512]{1,0:T(8,128)S(1)} %get-tuple-element.12.refs_0_, f32[1024,512]{1,0:T(8,128)S(1)} %get-tuple-element.13.refs_1_, f32[1024,512]{1,0:T(8,128)S(1)} %get-tuple-element.14.refs_2_, ...), custom_call_target="tpu_custom_call" | custom-call | tf_op jit(solution)/shard_map/store/pallas_call | solution.py:545
Async XLA Ops:
  1.3 249.7 %copy-start = (f32[1024,512]{1,0:T(8,128)S(1)}, f32[1024,512]{1,0:T(8,128)}, u32[]{:S(2)}) copy-start(f32[1024,512]{1,0:T(8,128)} %master.1) | copy-start | bytes 6291460
  1.3 249.7 %copy-start.1 = (f32[1024,512]{1,0:T(8,128)S(1)}, f32[1024,512]{1,0:T(8,128)}, u32[]{:S(2)}) copy-start(f32[1024,512]{1,0:T(8,128)} %mom1.1) | copy-start | bytes 6291460
  1.3 249.7 %copy-start.2 = (f32[1024,512]{1,0:T(8,128)S(1)}, f32[1024,512]{1,0:T(8,128)}, u32[]{:S(2)}) copy-start(f32[1024,512]{1,0:T(8,128)} %mom2.1) | copy-start | bytes 6291460
